TPU v7x, 32 devices: a whole 2x2x4 slice. The times are simulated.
32 devices in a mesh: group: 2 (over y), gx: 4 (over x, core), gy: 4 (over z).
Axes of the slice: x: 2, y: 2, z: 4, core: 2. Of those that a mesh axis runs over, the one named last changes fastest.
Arguments:
- pressure: float32 [192, 64, 768], P(('group', 'gx'), 'gy'), parts along dimension 0, may hold values from -6 to 6
- pressure_prev: float32 [192, 64, 768], P(('group', 'gx'), 'gy'), parts along dimension 0, may hold values from -6 to 6
- courant: float32 [192, 64, 768], P(('group', 'gx'), 'gy'), parts along dimension 0, may hold values from 0.05 to 0.3
- nonlinearity: float32 [192, 64, 768], P(('group', 'gx'), 'gy'), parts along dimension 0, may hold values from 0.03 to 0.3
- absorption: float32 [192, 64, 768], P(('group', 'gx'), 'gy'), parts along dimension 0, may hold values from 0.2 to 2
- own_map: int32 [96, 32], P(('group', 'gx'), 'gy'), parts along dimension 0, may hold values from 0 to 16, as said below
- slot_table: int32 [96, 32], P(('group', 'gx'), 'gy'), parts along dimension 0, may hold values from 0 to 511
- displacement: float32 [128, 128, 384], P(('group', 'gx'), 'gy'), parts along dimension 0, may hold values from -6 to 6
- displacement_prev: float32 [128, 128, 384], P(('group', 'gx'), 'gy'), parts along dimension 0, may hold values from -6 to 6
- layer_labels: int32 [128, 128, 384], P(('group', 'gx'), 'gy'), parts along dimension 0, may hold values from 0 to 3
- shear_table: float32 [8], P('group'), parts along dimension 0, may hold values from 0.05 to 0.15
- viscosity_table: float32 [8], P('group'), parts along dimension 0, may hold values from 0.01 to 0.06
Outputs:
- pressure_mid: float32 [192, 64, 768], P(('group', 'gx'), 'gy'), parts along dimension 0
- pressure_new: float32 [192, 64, 768], P(('group', 'gx'), 'gy'), parts along dimension 0
- tissue_force: float32 [128, 128, 384], P(('group', 'gx'), 'gy'), parts along dimension 0
- displacement_mid: float32 [128, 128, 384], P(('group', 'gx'), 'gy'), parts along dimension 0
- displacement_new: float32 [128, 128, 384], P(('group', 'gx'), 'gy'), parts along dimension 0
There are 2 independent parts, one for each index of `group`. A program takes and returns all parts, laid end to end along the dimension named above; each array names one. Nothing has to cross between parts.
Inputs may be any that keep to these rules, and one draw needn't show every extreme that they name: `own_map`: A value below 16 names tissue block (v // 4, v % 4); 16 marks a line outside the focal zone. Among the lines of one device's block of the map, at most 6 name any one tissue block, and exactly 6 do for some block in every draw.
All inputs are finite; a program needn't handle non-finite values.
Results may differ from a plain program's by a relative error of at most 0.0003.
Values sent between devices are 32-bit elements; how exact they have to be, the bound alone decides.
A program may use at most 64 MiB of HBM per device.

v0:
```python
import functools

import jax
import jax.numpy as jnp
from jax import lax
from jax.experimental import pallas as pl
from jax.experimental.pallas import tpu as pltpu
from jax.sharding import PartitionSpec as P

MESH = pl.DeviceIdType.MESH
F32 = jnp.float32
BF16 = jnp.bfloat16


def iota(shape, dim):
    return lax.broadcasted_iota(jnp.int32, shape, dim)


def split(x):
    high = x.astype(BF16)
    low = (x - high.astype(F32)).astype(BF16)
    return high, low


def dot(a, b):
    return jnp.dot(a, b, preferred_element_type=F32)


def laplace(centre, up, down, left, right):
    rows, lanes = centre.shape
    row, lane = iota(centre.shape, 0), iota(centre.shape, 1)
    xm = jnp.where(row == 0, left, pltpu.roll(centre, 1, 0))
    xp = jnp.where(row == rows - 1, right, pltpu.roll(centre, rows - 1, 0))
    ym = jnp.where(lane == 0, 0.0, pltpu.roll(centre, 1, 1))
    yp = jnp.where(lane == lanes - 1, 0.0, pltpu.roll(centre, lanes - 1, 1))
    return ((up + down) + (xm + xp)) + ((ym + yp) - 6.0 * centre)


class Faces:
    def __init__(self, axis, first, last, halo, send, recv, base):
        size, index = lax.axis_size(axis), lax.axis_index(axis)
        self.halo = halo
        self.has_next, self.has_prev = index < size - 1, index > 0
        self.up = pltpu.make_async_remote_copy(
            src_ref=last, dst_ref=halo.at[0], send_sem=send.at[base], recv_sem=recv.at[base],
            device_id={axis: lax.rem(index + 1, size)}, device_id_type=MESH)
        self.down = pltpu.make_async_remote_copy(
            src_ref=first, dst_ref=halo.at[1], send_sem=send.at[base + 1], recv_sem=recv.at[base + 1],
            device_id={axis: lax.rem(index + size - 1, size)}, device_id_type=MESH)

    def clear(self):
        @pl.when(jnp.logical_not(self.has_prev))
        def _():
            self.halo[0] = jnp.zeros(self.halo.shape[1:], F32)

        @pl.when(jnp.logical_not(self.has_next))
        def _():
            self.halo[1] = jnp.zeros(self.halo.shape[1:], F32)

    def start(self):
        pl.when(self.has_next)(self.up.start)
        pl.when(self.has_prev)(self.down.start)

    def wait(self):
        pl.when(self.has_prev)(self.up.wait_recv)
        pl.when(self.has_next)(self.down.wait_recv)

    def wait_send(self):
        pl.when(self.has_next)(self.up.wait_send)
        pl.when(self.has_prev)(self.down.wait_send)


def kernel(
    capacity, slots,
    p_in, q_in, c_in, n_in, a_in, own_in, slot_in, u_in, w_in, k_in, shear_in, viscosity_in,
    pm, pn, tf, um, rest, both, hz_out, hx_out,
    p, q, c, n, a, u, w, k, own, slot, shear_table, viscosity_table, load,
    hz_p, hx_p, fx_p, hz_m, hx_m, fx_m,
    hz_u, hx_u, fx_u, hz_w, hx_w, fx_w, hz_e, hx_e, fx_e,
    paired, packed, got, packed_places, got_places,
    send, recv, line_send, line_recv, place_send, place_recv,
):
    planes, rows, lateral = p.shape
    tile_rows, tile_cols, tile_depth = u.shape
    kinds = shear_table.shape[0]
    gx, gy = lax.axis_size("gx"), lax.axis_size("gy")
    blocks = gx * gy
    me = lax.axis_index("gx") * gy + lax.axis_index("gy")

    loads = [pltpu.make_async_copy(s, d, load.at[i]) for i, (s, d) in enumerate(
        ((p_in, p), (u_in, u), (w_in, w), (own_in, own), (slot_in, slot), (shear_in, shear_table),
         (viscosity_in, viscosity_table), (q_in, q), (c_in, c), (n_in, n), (a_in, a), (k_in, k)))]
    for copy in loads:
        copy.start()

    barrier = pltpu.get_barrier_semaphore()

    def greet(d, carry):
        other = lax.rem(me + d, blocks)
        pl.semaphore_signal(
            barrier, inc=1, device_id={"gx": other // gy, "gy": lax.rem(other, gy)}, device_id_type=MESH)
        return carry

    lax.fori_loop(1, blocks, greet, 0)

    def faces(first, last, halo, axis, base):
        return Faces(axis, first, last, halo, send, recv, base)

    def pair(field, hz, fx, hx, base):
        depth = field.shape[0]
        return (faces(field.at[0], field.at[depth - 1], hz, "gx", base),
                faces(fx.at[0], fx.at[1], hx, "gy", base + 2))

    p_z, p_x = pair(p, hz_p, fx_p, hx_p, 0)
    m_z, m_x = pair(pm, hz_m, fx_m, hx_m, 4)
    u_z, u_x = pair(u, hz_u, fx_u, hx_u, 8)
    w_z, w_x = pair(w, hz_w, fx_w, hx_w, 12)
    e_z, e_x = pair(um, hz_e, fx_e, hx_e, 16)
    every = (p_z, p_x, m_z, m_x, u_z, u_x, w_z, w_x, e_z, e_x)
    for item in every:
        item.clear()

    def stage(field, fx):
        def body(z, carry):
            plane = field[z]
            fx[0, pl.ds(z, 1), :] = plane[:1]
            fx[1, pl.ds(z, 1), :] = plane[-1:]
            return carry
        lax.fori_loop(0, field.shape[0], body, 0)

    loads[0].wait()
    stage(p, fx_p)
    pl.semaphore_wait(barrier, blocks - 1)
    p_z.start()
    p_x.start()
    loads[1].wait()
    loads[2].wait()
    stage(u, fx_u)
    stage(w, fx_w)
    u_z.start()
    u_x.start()
    w_z.start()
    w_x.start()

    loads[3].wait()
    loads[4].wait()

    lines_x, lines_z = own.shape
    count = lines_z * rows
    padded = -(-count // 128) * 128

    def along_lanes(table):
        column = iota((lines_x, padded), 1)
        here = lax.rem(column, rows) // 2 == iota((lines_x, padded), 0)
        total = jnp.zeros((lines_x, padded), F32)
        for z in range(lines_z):
            total = total + jnp.where(here & (column // rows == z), table[:, z:z + 1], 0.0)
        return jnp.sum(total, axis=0, keepdims=True)

    owners = own[...].astype(F32)
    owner_lane = along_lanes(owners)
    owner_row = jnp.transpose(jnp.broadcast_to(owner_lane, (128, padded)))[:count, :1]
    owner_lane = owner_lane[:, :count]
    place_lane = along_lanes(slot[...].astype(F32))[:, :count]
    earlier = iota((count, count), 0) // 2 < iota((count, count), 1) // 2
    rank = 0.5 * jnp.sum(
        jnp.where((owner_row == owner_lane) & earlier, 1.0, 0.0), axis=0, keepdims=True)
    target = owner_lane * float(slots) + rank
    match = iota((blocks * slots, count), 0).astype(F32) == target
    even = lax.rem(iota((blocks * slots, count), 1), 2) == 0
    places = jnp.sum(jnp.where(match & even, place_lane + 1.0, 0.0), axis=1, keepdims=True)
    packed_places[...] = jnp.broadcast_to(places, packed_places.shape)
    match = jnp.where(match, 1.0, 0.0).astype(BF16)

    def sends(source, target_ref, send_sems, recv_sems):
        def copy(d):
            other = lax.rem(me + d, blocks)
            return pltpu.make_async_remote_copy(
                src_ref=source.at[pl.ds(pl.multiple_of(other * slots, slots), slots)],
                dst_ref=target_ref.at[pl.ds(pl.multiple_of(me * slots, slots), slots)],
                send_sem=send_sems.at[d], recv_sem=recv_sems.at[d],
                device_id={"gx": other // gy, "gy": lax.rem(other, gy)}, device_id_type=MESH)

        def start():
            lax.fori_loop(1, blocks, lambda d, carry: (copy(d).start(), carry)[1], 0)
            here = pl.ds(pl.multiple_of(me * slots, slots), slots)
            target_ref[here, :] = source[here, :]

        def wait():
            lax.fori_loop(1, blocks, lambda d, carry: (copy(d).wait_recv(), carry)[1], 0)

        def wait_send():
            lax.fori_loop(1, blocks, lambda d, carry: (copy(d).wait_send(), carry)[1], 0)

        return start, wait, wait_send

    start_places, wait_places, wait_places_send = sends(packed_places, got_places, place_send, place_recv)
    start_lines, wait_lines, wait_lines_send = sends(packed, got, line_send, line_recv)
    start_places()

    def wave(now, before, lap, z):
        return (2.0 * now - before + c[z] * lap + n[z] * (now * now - before * before)
                - 0.1 * a[z] * (now - before))

    def first(z, up, down):
        now = p[z]
        lap = laplace(now, up, down, hx_p[0, pl.ds(z, 1), :], hx_p[1, pl.ds(z, 1), :])
        mid = wave(now, q[z], lap, z)
        pm[z] = mid
        fx_m[0, pl.ds(z, 1), :] = mid[:1]
        fx_m[1, pl.ds(z, 1), :] = mid[-1:]

    for copy in loads[7:11]:
        copy.wait()
    p_z.wait()
    p_x.wait()
    first(0, hz_p[0], p[1])
    first(planes - 1, p[planes - 2], hz_p[1])
    m_z.start()
    lax.fori_loop(1, planes - 1, lambda z, carry: (first(z, p[z - 1], p[z + 1]), carry)[1], 0)
    m_x.start()

    loads[5].wait()
    loads[6].wait()
    loads[11].wait()
    for item in (u_z, u_x, w_z, w_x):
        item.wait()

    def elastic(z, u_up, u_down, w_up, w_down):
        now, before, kind = u[z], w[z], k[z]
        lap_u = laplace(now, u_up, u_down, hx_u[0, pl.ds(z, 1), :], hx_u[1, pl.ds(z, 1), :])
        lap_w = laplace(before, w_up, w_down, hx_w[0, pl.ds(z, 1), :], hx_w[1, pl.ds(z, 1), :])
        shear, viscosity = jnp.zeros(now.shape, F32), jnp.zeros(now.shape, F32)
        for i in range(kinds):
            shear = jnp.where(kind == i, shear_table[i], shear)
            viscosity = jnp.where(kind == i, viscosity_table[i], viscosity)
        um[z] = 2.0 * now - before + shear * lap_u + viscosity * (lap_u - lap_w)
        rest[z] = now + viscosity * lap_u
        both[z] = shear + viscosity

    elastic(0, hz_u[0], u[1], hz_w[0], w[1])
    elastic(tile_rows - 1, u[tile_rows - 2], hz_u[1], w[tile_rows - 2], hz_w[1])
    lax.fori_loop(1, tile_rows - 1, lambda z, carry: (
        elastic(z, u[z - 1], u[z + 1], w[z - 1], w[z + 1]), carry)[1], 0)

    def second(z, up, down):
        now = pm[z]
        lap = laplace(now, up, down, hx_m[0, pl.ds(z, 1), :], hx_m[1, pl.ds(z, 1), :])
        new = wave(now, p[z], lap, z)
        pn[z] = new
        return 0.1 * a[z] * (now * now + new * new) * lax.rsqrt(c[z])

    def pair_at(i):
        return pl.ds(pl.multiple_of(i * rows, rows), rows)

    m_z.wait()
    m_x.wait()
    paired[pair_at(0), :] = second(0, hz_m[0], pm[1]) + second(1, pm[0], pm[2])
    last = planes // 2 - 1
    paired[pair_at(last), :] = second(planes - 2, pm[planes - 3], pm[planes - 1]) + second(
        planes - 1, pm[planes - 2], hz_m[1])

    def two(i, carry):
        z = 2 * i
        paired[pair_at(i), :] = second(z, pm[z - 1], pm[z + 1]) + second(z + 1, pm[z], pm[z + 2])
        return carry

    lax.fori_loop(1, last, two, 0)

    width = 256
    half = width // 2
    lanes_two = jnp.where(iota((width, half), 0) // 2 == iota((width, half), 1), 0.125, 0.0).astype(BF16)
    for i in range(lateral // width):
        high, low = split(paired[:, i * width:(i + 1) * width])
        coarse = dot(high, lanes_two) + dot(low, lanes_two)
        high, low = split(coarse)
        packed[:, i * half:(i + 1) * half] = dot(match, high) + dot(match, low)
    start_lines()

    wait_places()
    spots = jnp.transpose(got_places[...])[:1] - 1.0
    cells = tile_rows * tile_cols
    landing = jnp.where(
        iota((cells, blocks * slots), 0).astype(F32) == spots, 1.0, 0.0).astype(BF16)
    wait_lines()
    high, low = split(got[...])
    chunk = 4 if tile_rows % 4 == 0 else 1
    for r in range(0, tile_rows, chunk):
        part = landing[r * tile_cols:(r + chunk) * tile_cols]
        force = (dot(part, high) + dot(part, low)).reshape(chunk, tile_cols, tile_depth)
        tf[r:r + chunk] = force
        mid = um[r:r + chunk] + 0.25 * force
        um[r:r + chunk] = mid
        for j in range(chunk):
            fx_e[0, r + j:r + j + 1, :] = mid[j, :1]
            fx_e[1, r + j:r + j + 1, :] = mid[j, -1:]
    e_z.start()
    e_x.start()
    e_z.wait()
    e_x.wait()

    hz_out[...] = hz_e[...]
    hx_out[...] = hx_e[...]
    for item in every:
        item.wait_send()
    wait_places_send()
    wait_lines_send()


def finish(pm, pn, tf, um, rest, both, hz, hx, pm_out, pn_out, tf_out, um_out, un_out, un, sems):
    copies = [pltpu.make_async_copy(s, d, sems.at[i]) for i, (s, d) in enumerate(
        ((pm, pm_out), (pn, pn_out), (tf, tf_out), (um, um_out)))]
    for copy in copies:
        copy.start()
    tile_rows = um.shape[0]

    def final(z, up, down):
        now = um[z]
        lap = laplace(now, up, down, hx[0, pl.ds(z, 1), :], hx[1, pl.ds(z, 1), :])
        un[z] = 2.0 * now - rest[z] + both[z] * lap + 0.25 * tf[z]

    final(0, hz[0], um[1])
    final(tile_rows - 1, um[tile_rows - 2], hz[1])
    lax.fori_loop(1, tile_rows - 1, lambda z, carry: (final(z, um[z - 1], um[z + 1]), carry)[1], 0)
    copies.append(pltpu.make_async_copy(un, un_out, sems.at[4]))
    copies[4].start()
    for copy in copies:
        copy.wait()


def local(pressure, pressure_prev, courant, nonlinearity, absorption, own_map, slot_table,
          displacement, displacement_prev, layer_labels, shear_table, viscosity_table):
    planes, rows, lateral = pressure.shape
    tile = displacement.shape
    blocks = lax.axis_size("gx") * lax.axis_size("gy")
    capacity = max(2, own_map.shape[0] * own_map.shape[1] // blocks)
    slots = -(-capacity // 8) * 8
    hbm = pl.BlockSpec(memory_space=pltpu.HBM)
    vmem = pl.BlockSpec(memory_space=pltpu.VMEM)
    wave, cell = pltpu.VMEM(pressure.shape, F32), pltpu.VMEM(tile, F32)

    def halos(shape):
        z, x = pltpu.VMEM((2,) + shape[1:], F32), pltpu.VMEM((2, shape[0], shape[2]), F32)
        return [z, x, x]

    dma = pltpu.SemaphoreType.DMA
    kinds = shear_table.shape[0]
    lines = pltpu.VMEM(own_map.shape[::-1], jnp.int32)
    waves = [jax.ShapeDtypeStruct(pressure.shape, F32)] * 2
    cells = [jax.ShapeDtypeStruct(tile, F32)]
    parts = pl.pallas_call(
        functools.partial(kernel, capacity, slots),
        out_shape=[wave] * 2 + [cell] * 4 + [pltpu.VMEM((2,) + tile[1:], F32),
                                             pltpu.VMEM((2, tile[0], tile[2]), F32)],
        in_specs=[hbm] * 12,
        out_specs=[vmem] * 8,
        scratch_shapes=[wave] * 5 + [cell] * 2 + [
            pltpu.VMEM(tile, jnp.int32), lines, lines,
            pltpu.SMEM((kinds,), F32), pltpu.SMEM((kinds,), F32), dma((12,))]
        + halos(pressure.shape) * 2 + halos(tile) * 3
        + [pltpu.VMEM((planes // 2 * rows, lateral), F32),
           pltpu.VMEM((blocks * slots, lateral // 2), F32),
           pltpu.VMEM((blocks * slots, lateral // 2), F32),
           pltpu.VMEM((blocks * slots, 128), F32),
           pltpu.VMEM((blocks * slots, 128), F32),
           dma((20,)), dma((20,)), dma((blocks,)), dma((blocks,)), dma((blocks,)), dma((blocks,))],
        compiler_params=pltpu.CompilerParams(
            collective_id=0, has_side_effects=True, vmem_limit_bytes=58 * 1024 * 1024),
    )(pressure, pressure_prev, courant, nonlinearity, absorption, own_map.T, slot_table.T,
      displacement, displacement_prev, layer_labels, shear_table, viscosity_table)
    return pl.pallas_call(
        finish,
        out_shape=waves + cells * 3,
        in_specs=[vmem] * 8,
        out_specs=[hbm] * 5,
        scratch_shapes=[cell, dma((5,))],
        compiler_params=pltpu.CompilerParams(vmem_limit_bytes=40 * 1024 * 1024),
    )(*parts)


def solution(mesh):
    field = P(("group", "gx"), "gy", None)
    table = P(("group", "gx"), "gy")
    return jax.shard_map(
        local,
        mesh=mesh,
        in_specs=(field,) * 5 + (table,) * 2 + (field,) * 3 + (P("group"),) * 2,
        out_specs=(field,) * 5,
        check_vma=False,
    )
```

profile of v0, /device:TPU:0, one launch (start us, length us, event | category | flops | bytes accessed | tf_op | source)
XLA Modules:
  0.0 31.0 jit_solution(8627930961873646363)
XLA Ops:
  0.6 27.8 %shard_map.155 = (f32[24,16,768]{2,1,0:T(8,128)S(1)}, f32[24,16,768]{2,1,0:T(8,128)S(1)}, f32[16,32,384]{2,1,0:T(8,128)S(1)}, f32[16,32,384]{2,1,0:T(8,128)S(1)}...) custom-call(f32[24,16,768]{2,1,0:T(8,128)} %p_in.1, ...), custom_call_target="tpu_custom_call" | custom-call | tf_op jit(solution)/shard_map/pallas_call | solution.py:351
  28.4 2.5 %shard_map.156 = (f32[24,16,768]{2,1,0:T(8,128)}, f32[24,16,768]{2,1,0:T(8,128)}, f32[16,32,384]{2,1,0:T(8,128)}, f32[16,32,384]{2,1,0:T(8,128)}, f32[16,32,384]{2,1,0:T(8,128)}) custom-call(f32[24,16,768]{2,1,0:T(8,128)S(1)} %get-tuple-element.13.pm, f32[24,16,768]{2,1,0:T(8,128)S(1)} %get-tuple-element.14.pn, f32[16,32,384]{2,1,0:T(8,128)S(1)} %get-tuple-element.15.tf, ...), custom_call_target="tpu_custom_call" | custom-call | tf_op jit(solution)/shard_map/pallas_call | solution.py:371
where the time goes:
time: 31.1 us; the launch traced here: 31 us
  Pallas kernels  30.3 us (97%)
  between operations  0.64 us (2%)
    pallas_call x1, Pallas kernels, local(): pl.pallas_call(functools.partial(kernel, capacity, slots), out_shape=[wav...  27.8 us
    pallas_call x1, Pallas kernels, local(): pl.pallas_call(finish, out_shape=waves + cells * 3, in_specs=[vmem] * 8,...  2.53 us

commit v1 on v0

v1 whole, which is shorter than its diff:
```python
import functools

import jax
import jax.numpy as jnp
from jax import lax
from jax.experimental import pallas as pl
from jax.experimental.pallas import tpu as pltpu
from jax.sharding import PartitionSpec as P

MESH = pl.DeviceIdType.MESH
F32 = jnp.float32
BF16 = jnp.bfloat16


def iota(shape, dim):
    return lax.broadcasted_iota(jnp.int32, shape, dim)


def split(x):
    high = x.astype(BF16)
    low = (x - high.astype(F32)).astype(BF16)
    return high, low


def dot(a, b):
    return jnp.dot(a, b, preferred_element_type=F32)


def laplace(centre, up, down, left=0.0, right=0.0):
    rows, lanes = centre.shape
    row, lane = iota(centre.shape, 0), iota(centre.shape, 1)
    xm = jnp.where(row == 0, left, pltpu.roll(centre, 1, 0))
    xp = jnp.where(row == rows - 1, right, pltpu.roll(centre, rows - 1, 0))
    ym = jnp.where(lane == 0, 0.0, pltpu.roll(centre, 1, 1))
    yp = jnp.where(lane == lanes - 1, 0.0, pltpu.roll(centre, lanes - 1, 1))
    if up is None:
        beside = down
    elif down is None:
        beside = up
    else:
        beside = up + down
    return (beside + (xm + xp)) + ((ym + yp) - 6.0 * centre)


class Faces:
    def __init__(self, axis, pieces, halo, send, recv, base):
        size, index = lax.axis_size(axis), lax.axis_index(axis)
        self.halo = halo
        self.has_next, self.has_prev = index < size - 1, index > 0
        self.up, self.down = [], []
        for i, (first, last, part) in enumerate(pieces):
            at = base + 2 * i
            self.up.append(pltpu.make_async_remote_copy(
                src_ref=last, dst_ref=part(halo, 0), send_sem=send.at[at], recv_sem=recv.at[at],
                device_id={axis: lax.rem(index + 1, size)}, device_id_type=MESH))
            self.down.append(pltpu.make_async_remote_copy(
                src_ref=first, dst_ref=part(halo, 1), send_sem=send.at[at + 1], recv_sem=recv.at[at + 1],
                device_id={axis: lax.rem(index + size - 1, size)}, device_id_type=MESH))

    def clear(self):
        @pl.when(jnp.logical_not(self.has_prev))
        def _():
            self.halo[0] = jnp.zeros(self.halo.shape[1:], F32)

        @pl.when(jnp.logical_not(self.has_next))
        def _():
            self.halo[1] = jnp.zeros(self.halo.shape[1:], F32)

    def start(self, i=0):
        pl.when(self.has_next)(self.up[i].start)
        pl.when(self.has_prev)(self.down[i].start)

    def wait(self, i=0):
        pl.when(self.has_prev)(self.up[i].wait_recv)
        pl.when(self.has_next)(self.down[i].wait_recv)

    def wait_send(self):
        @pl.when(self.has_next)
        def _():
            for copy in self.up:
                copy.wait_send()

        @pl.when(self.has_prev)
        def _():
            for copy in self.down:
                copy.wait_send()


def kernel(
    capacity, slots, width,
    p_in, q_in, c_in, n_in, a_in, own_in, slot_in, u_in, w_in, k_in, shear_in, viscosity_in,
    pm, pn, tf, um, un, both, hz_out, hx_out,
    p, q, c, n, a, u, w, k, own, slot, shear_table, viscosity_table, load,
    fz_p, fx_p, fx_c, fx_a, fx_m, fx_n, fz_e, fx_e,
    hz_p, hx_p, hz_m, hx_m, hz_u, hx_u, hz_w, hx_w, hz_e, hx_e,
    rest, paired, gain, packed, got, packed_places, got_places,
    send, recv, line_send, line_recv, place_send, place_recv,
):
    planes, rows, lateral = p.shape
    tile_rows, tile_cols, tile_depth = u.shape
    kinds = shear_table.shape[0]
    half = width // 2
    chunks = lateral // width
    gx, gy = lax.axis_size("gx"), lax.axis_size("gy")
    blocks = gx * gy
    me = lax.axis_index("gx") * gy + lax.axis_index("gy")

    barrier = pltpu.get_barrier_semaphore()

    def greet(d, carry):
        other = lax.rem(me + d, blocks)
        pl.semaphore_signal(
            barrier, inc=1, device_id={"gx": other // gy, "gy": lax.rem(other, gy)}, device_id_type=MESH)
        return carry

    cuts = 3 if planes % 3 == 0 else 1
    step = planes // cuts

    def load_of(pairs, base):
        return [pltpu.make_async_copy(s, d, load.at[base + i]) for i, (s, d) in enumerate(pairs)]

    faces_in = load_of((
        (p_in.at[:, 0, :], fx_p.at[0]), (p_in.at[:, rows - 1, :], fx_p.at[1]),
        (p_in.at[0], fz_p.at[0]), (p_in.at[planes - 1], fz_p.at[1])), 0)
    waves_in = [load_of([(s.at[pl.ds(i * step, step)], d.at[pl.ds(i * step, step)]) for s, d in (
        (p_in, p), (q_in, q), (c_in, c), (n_in, n), (a_in, a))], 4 + 5 * i) for i in range(cuts)]
    base = 4 + 5 * cuts
    table_in = load_of(((own_in, own), (slot_in, slot)), base)
    sides_in = load_of((
        (c_in.at[:, 0, :], fx_c.at[0]), (c_in.at[:, rows - 1, :], fx_c.at[1]),
        (a_in.at[:, 0, :], fx_a.at[0]), (a_in.at[:, rows - 1, :], fx_a.at[1])), base + 2)
    cells_in = load_of((
        (u_in, u), (w_in, w), (k_in, k), (shear_in, shear_table), (viscosity_in, viscosity_table)), base + 6)

    for copy in faces_in:
        copy.start()
    lax.fori_loop(1, blocks, greet, 0)
    for copy in table_in:
        copy.start()
    for group in waves_in:
        for copy in group:
            copy.start()
    for copy in sides_in + cells_in:
        copy.start()

    def lanes(i):
        return slice(i * width, (i + 1) * width)

    def depths(i):
        return slice(i * half, (i + 1) * half)

    def whole(halo, side):
        return halo.at[side]

    def cut(at):
        return lambda halo, side: halo.at[side, :, at]

    def cut_all(first, last, at):
        return [(first.at[:, at(i)], last.at[:, at(i)], cut(at(i))) for i in range(chunks)]

    p_z = Faces("gx", cut_all(fz_p.at[0], fz_p.at[1], lanes), hz_p, send, recv, 0)
    p_x = Faces("gy", cut_all(fx_p.at[0], fx_p.at[1], lanes), hx_p, send, recv, 2 * chunks)
    m_z = Faces("gx", cut_all(pm.at[0], pm.at[planes - 1], lanes), hz_m, send, recv, 4 * chunks)
    m_x = Faces("gy", cut_all(fx_m.at[0], fx_m.at[1], lanes), hx_m, send, recv, 6 * chunks)
    e_z = Faces("gx", cut_all(fz_e.at[0], fz_e.at[1], depths), hz_e, send, recv, 8 * chunks)
    e_x = Faces("gy", cut_all(fx_e.at[0], fx_e.at[1], depths), hx_e, send, recv, 10 * chunks)
    rest_at = 12 * chunks
    u_z = Faces("gx", [(u_in.at[0], u_in.at[tile_rows - 1], whole)], hz_u, send, recv, rest_at)
    u_x = Faces("gy", [(u_in.at[:, 0, :], u_in.at[:, tile_cols - 1, :], whole)], hx_u, send, recv, rest_at + 2)
    w_z = Faces("gx", [(w_in.at[0], w_in.at[tile_rows - 1], whole)], hz_w, send, recv, rest_at + 4)
    w_x = Faces("gy", [(w_in.at[:, 0, :], w_in.at[:, tile_cols - 1, :], whole)], hx_w, send, recv, rest_at + 6)
    every = (p_z, p_x, m_z, m_x, u_z, u_x, w_z, w_x, e_z, e_x)

    for copy in faces_in:
        copy.wait()
    pl.semaphore_wait(barrier, blocks - 1)
    for i in range(chunks):
        p_x.start(i)
        p_z.start(i)
    for item in (u_x, w_x, u_z, w_z):
        item.start()
    for item in every:
        item.clear()

    for copy in table_in:
        copy.wait()
    lines_x, lines_z = own.shape
    count = lines_z * rows
    total = count + 2 * planes
    padded = -(-total // 128) * 128

    def line_of(column):
        beyond = column - count
        side = jnp.where(beyond >= planes, 1, 0)
        x = jnp.where(column < count, lax.rem(column, rows) // 2, side * (lines_x - 1))
        z = jnp.where(column < count, column // rows, (beyond - side * planes) // 2)
        return z, x

    def along_lanes(table):
        z_of, x_of = line_of(iota((lines_x, padded), 1))
        here = x_of == iota((lines_x, padded), 0)
        result = jnp.zeros((lines_x, padded), F32)
        for z in range(lines_z):
            result = result + jnp.where(here & (z_of == z), table[:, z:z + 1], 0.0)
        return jnp.sum(result, axis=0, keepdims=True)

    owners = own[...].astype(F32)
    owner_lane = along_lanes(owners)
    owner_row = jnp.transpose(jnp.broadcast_to(owner_lane, (128, padded)))[:count, :1]
    owner_lane = owner_lane[:, :total]
    place_lane = along_lanes(slot[...].astype(F32))[:, :total]
    z_of, x_of = line_of(iota((count, total), 1))
    earlier = iota((count, total), 0) // 2 < z_of * lines_x + x_of
    rank = 0.5 * jnp.sum(
        jnp.where((owner_row == owner_lane) & earlier, 1.0, 0.0), axis=0, keepdims=True)
    target = owner_lane * float(slots) + rank
    match = iota((blocks * slots, total), 0).astype(F32) == target
    column = iota((blocks * slots, total), 1)
    counted = (lax.rem(column, 2) == 0) & (column < count)
    places = jnp.sum(jnp.where(match & counted, place_lane + 1.0, 0.0), axis=1, keepdims=True)
    aligned = lax.rem(iota((blocks * slots, 128), 0), slots) == lax.rem(iota((blocks * slots, 128), 1), slots)
    places = jnp.where(aligned, places, 0.0).reshape(blocks, slots, 128)
    packed_places[...] = jnp.sum(places, axis=1, keepdims=True)
    match = jnp.where(match, 1.0, 0.0).astype(BF16)

    def at_block(other):
        return {"gx": other // gy, "gy": lax.rem(other, gy)}

    def each(start):
        lax.fori_loop(1, blocks, lambda d, carry: (start(lax.rem(me + d, blocks)), carry)[1], 0)

    def place_copy(source, target_ref, device):
        return pltpu.make_async_remote_copy(
            src_ref=source, dst_ref=target_ref, send_sem=place_send.at[0], recv_sem=place_recv.at[0],
            device_id=at_block(device), device_id_type=MESH)

    def line_copy(i, source, target_ref, device):
        return pltpu.make_async_remote_copy(
            src_ref=source, dst_ref=target_ref, send_sem=line_send.at[i], recv_sem=line_recv.at[i],
            device_id=at_block(device), device_id_type=MESH)

    used = pl.ds(0, capacity)
    others = pl.ds(0, blocks - 1)

    def start_places():
        each(lambda other: place_copy(packed_places.at[other], got_places.at[me], other).start())
        got_places[me] = packed_places[me]

    def start_lines(i):
        each(lambda other: line_copy(
            i, packed.at[i, other, used], got.at[i, me, used], other).start())
        got[i, me] = packed[i, me]

    all_places = place_copy(packed_places.at[others], got_places.at[others], 0)
    all_lines = [line_copy(i, packed.at[i, others, used], got.at[i, others, used], 0) for i in range(chunks)]

    start_places()

    def wave(now, before, lap, z):
        return (2.0 * now - before + c[z] * lap + n[z] * (now * now - before * before)
                - 0.1 * a[z] * (now - before))

    def first(z, up, down):
        now = p[z]
        mid = wave(now, q[z], laplace(now, up, down), z)
        pm[z] = mid
        fx_m[0, pl.ds(z, 1), :] = mid[:1]
        fx_m[1, pl.ds(z, 1), :] = mid[-1:]

    for i, group in enumerate(waves_in):
        for copy in group:
            copy.wait()
        low, high = i * step - 1, (i + 1) * step - 1
        if i == 0:
            first(0, None, p[1])
            low = 1
        if i == cuts - 1:
            high = planes - 1
        lax.fori_loop(low, high, lambda z, carry: (first(z, p[z - 1], p[z + 1]), carry)[1], 0)
        if i == cuts - 1:
            first(planes - 1, p[planes - 2], None)
    for copy in sides_in:
        copy.wait()

    for i in range(chunks):
        at = lanes(i)
        p_x.wait(i)
        p_z.wait(i)
        top = c[0, :, at] * hz_p[0, :, at]
        bottom = c[planes - 1, :, at] * hz_p[1, :, at]
        pm[0, :, at] = pm[0, :, at] + top
        pm[planes - 1, :, at] = pm[planes - 1, :, at] + bottom
        z = iota((planes, width), 0)
        for side, row in ((0, 0), (1, rows - 1)):
            extra = fx_c[side, :, at] * hx_p[side, :, at]
            extra = extra + jnp.where(z == 0, top[row:row + 1], 0.0)
            extra = extra + jnp.where(z == planes - 1, bottom[row:row + 1], 0.0)
            mid = fx_m[side, :, at] + extra
            fx_m[side, :, at] = mid
            pm[:, row, at] = mid
        m_x.start(i)
        m_z.start(i)

    def second(z, up, down):
        now = pm[z]
        new = wave(now, p[z], laplace(now, up, down), z)
        pn[z] = new
        fx_n[0, pl.ds(z, 1), :] = new[:1]
        fx_n[1, pl.ds(z, 1), :] = new[-1:]
        return 0.1 * a[z] * (now * now + new * new) * lax.rsqrt(c[z])

    def pair_at(i):
        return pl.ds(pl.multiple_of(i * rows, rows), rows)

    paired[pair_at(0), :] = second(0, None, pm[1]) + second(1, pm[0], pm[2])
    last = planes // 2 - 1

    def two(i, carry):
        z = 2 * i
        paired[pair_at(i), :] = second(z, pm[z - 1], pm[z + 1]) + second(z + 1, pm[z], pm[z + 2])
        return carry

    lax.fori_loop(1, last, two, 0)
    paired[pair_at(last), :] = second(planes - 2, pm[planes - 3], pm[planes - 1]) + second(
        planes - 1, pm[planes - 2], None)
    gain[...] = 0.1 * fx_a[...] * lax.rsqrt(fx_c[...])

    lanes_two = jnp.where(iota((width, half), 0) // 2 == iota((width, half), 1), 0.125, 0.0).astype(BF16)
    for i in range(chunks):
        at = lanes(i)
        m_x.wait(i)
        m_z.wait(i)
        for side, z, pair in ((0, 0, 0), (1, planes - 1, last)):
            old = pn[z, :, at]
            extra = c[z, :, at] * hz_m[side, :, at]
            new = old + extra
            pn[z, :, at] = new
            fx_n[0, z:z + 1, at] = new[:1]
            fx_n[1, z:z + 1, at] = new[-1:]
            where = slice(pair * rows, (pair + 1) * rows)
            paired[where, at] = paired[where, at] + (
                0.1 * a[z, :, at] * lax.rsqrt(c[z, :, at]) * (extra * (2.0 * old + extra)))
        for side in range(2):
            old = fx_n[side, :, at]
            extra = fx_c[side, :, at] * hx_m[side, :, at]
            fx_n[side, :, at] = old + extra
            paired[count + side * planes:count + (side + 1) * planes, at] = (
                gain[side, :, at] * (extra * (2.0 * old + extra)))
        high, low = split(paired[:, at])
        coarse = dot(high, lanes_two) + dot(low, lanes_two)
        high, low = split(coarse)
        packed[i] = (dot(match, high) + dot(match, low)).reshape(blocks, slots, half)
        start_lines(i)

    for side, row in ((0, 0), (1, rows - 1)):
        pn[:, row, :] = fx_n[side]

    for copy in cells_in:
        copy.wait()
    for item in (u_z, u_x, w_z, w_x):
        item.wait()

    def elastic(z, u_up, u_down, w_up, w_down):
        now, before, kind = u[z], w[z], k[z]
        lap_u = laplace(now, u_up, u_down, hx_u[0, pl.ds(z, 1), :], hx_u[1, pl.ds(z, 1), :])
        lap_w = laplace(before, w_up, w_down, hx_w[0, pl.ds(z, 1), :], hx_w[1, pl.ds(z, 1), :])
        shear, viscosity = jnp.zeros(now.shape, F32), jnp.zeros(now.shape, F32)
        for i in range(kinds):
            shear = jnp.where(kind == i, shear_table[i], shear)
            viscosity = jnp.where(kind == i, viscosity_table[i], viscosity)
        mid = 2.0 * now - before + shear * lap_u + viscosity * (lap_u - lap_w)
        um[z] = mid
        fx_e[0, pl.ds(z, 1), :] = mid[:1]
        fx_e[1, pl.ds(z, 1), :] = mid[-1:]
        rest[z] = now + viscosity * lap_u
        both[z] = shear + viscosity

    elastic(0, hz_u[0], u[1], hz_w[0], w[1])
    elastic(tile_rows - 1, u[tile_rows - 2], hz_u[1], w[tile_rows - 2], hz_w[1])
    lax.fori_loop(1, tile_rows - 1, lambda z, carry: (
        elastic(z, u[z - 1], u[z + 1], w[z - 1], w[z + 1]), carry)[1], 0)

    all_places.wait_recv()
    spread = -(-blocks * slots // 128)
    sources = jnp.concatenate([got_places[:, 0, :]] * spread, axis=1)[:, :blocks * slots]
    mine = iota((blocks, blocks * slots), 1) // slots == iota((blocks, blocks * slots), 0)
    spots = jnp.sum(jnp.where(mine, sources, 0.0), axis=0, keepdims=True) - 1.0
    cells = tile_rows * tile_cols

    def landing_of(cell):
        return jnp.where(cell.astype(F32) == spots, 1.0, 0.0).astype(BF16)

    landing = landing_of(iota((cells, blocks * slots), 0))
    edges = 2 * tile_cols + 2 * tile_rows
    edge = iota((edges, blocks * slots), 0)
    beyond = edge - 2 * tile_cols
    edge_landing = landing_of(jnp.where(
        edge < tile_cols, edge, jnp.where(
            edge < 2 * tile_cols, edge + (cells - 2 * tile_cols), jnp.where(
                beyond < tile_rows, beyond * tile_cols, (beyond - tile_rows) * tile_cols + tile_cols - 1))))
    real = lax.rem(iota((blocks * slots, half), 0), slots) < capacity

    chunk = 4 if tile_rows % 4 == 0 else 1
    for i in range(chunks):
        at = depths(i)
        all_lines[i].wait_recv()
        lines = jnp.where(real, got[i].reshape(blocks * slots, half), 0.0)
        parts = jnp.concatenate(split(lines), axis=1)

        def sums(where):
            result = dot(where, parts)
            return result[:, :half] + result[:, half:]

        edge_force = 0.25 * sums(edge_landing)
        for side, z in ((0, 0), (1, tile_rows - 1)):
            fz_e[side, :, at] = um[z, :, at] + edge_force[side * tile_cols:(side + 1) * tile_cols]
            here = 2 * tile_cols + side * tile_rows
            fx_e[side, :, at] = fx_e[side, :, at] + edge_force[here:here + tile_rows]
        e_x.start(i)
        e_z.start(i)
        for r in range(0, tile_rows, chunk):
            force = sums(landing[r * tile_cols:(r + chunk) * tile_cols]).reshape(chunk, tile_cols, half)
            tf[r:r + chunk, :, at] = force
            um[r:r + chunk, :, at] = um[r:r + chunk, :, at] + 0.25 * force

    def final(z, up, down):
        now = um[z]
        un[z] = 2.0 * now - rest[z] + both[z] * laplace(now, up, down) + 0.25 * tf[z]

    final(0, None, um[1])
    final(tile_rows - 1, um[tile_rows - 2], None)
    lax.fori_loop(1, tile_rows - 1, lambda z, carry: (final(z, um[z - 1], um[z + 1]), carry)[1], 0)

    for item in every[:-2]:
        item.wait_send()
    all_places.wait_send()
    for item in all_lines:
        item.wait_send()
    for i in range(chunks):
        e_z.wait(i)
        e_x.wait(i)
    hz_out[...] = hz_e[...]
    hx_out[...] = hx_e[...]
    e_z.wait_send()
    e_x.wait_send()


def finish(pm, pn, tf, um, partial, both, hz, hx, pm_out, pn_out, tf_out, um_out, un_out, un, sems):
    copies = [pltpu.make_async_copy(s, d, sems.at[i]) for i, (s, d) in enumerate(
        ((pm, pm_out), (pn, pn_out), (tf, tf_out), (um, um_out)))]
    for copy in copies:
        copy.start()
    tile_rows, tile_cols, _ = um.shape

    def final(z, carry):
        scale = both[z]
        row = iota(scale.shape, 0)
        extra = jnp.where(row == 0, hx[0, pl.ds(z, 1), :], 0.0) + jnp.where(
            row == tile_cols - 1, hx[1, pl.ds(z, 1), :], 0.0)
        un[z] = partial[z] + scale * extra
        return carry

    lax.fori_loop(0, tile_rows, final, 0)
    for side, z in ((0, 0), (1, tile_rows - 1)):
        un[z] = un[z] + both[z] * hz[side]
    copies.append(pltpu.make_async_copy(un, un_out, sems.at[4]))
    copies[4].start()
    for copy in copies:
        copy.wait()


def local(pressure, pressure_prev, courant, nonlinearity, absorption, own_map, slot_table,
          displacement, displacement_prev, layer_labels, shear_table, viscosity_table):
    planes, rows, lateral = pressure.shape
    tile = displacement.shape
    blocks = lax.axis_size("gx") * lax.axis_size("gy")
    capacity = max(2, own_map.shape[0] * own_map.shape[1] // blocks)
    slots = -(-capacity // 8) * 8
    width = 256
    chunks = lateral // width
    hbm = pl.BlockSpec(memory_space=pltpu.HBM)
    vmem = pl.BlockSpec(memory_space=pltpu.VMEM)
    wave, cell = pltpu.VMEM(pressure.shape, F32), pltpu.VMEM(tile, F32)

    def along_z(shape):
        return pltpu.VMEM((2,) + shape[1:], F32)

    def along_x(shape):
        return pltpu.VMEM((2, shape[0], shape[2]), F32)

    dma = pltpu.SemaphoreType.DMA
    kinds = shear_table.shape[0]
    table = pltpu.VMEM(own_map.shape[::-1], jnp.int32)
    wave_z, wave_x, cell_z, cell_x = along_z(pressure.shape), along_x(pressure.shape), along_z(tile), along_x(tile)
    lines = pltpu.VMEM((chunks, blocks, slots, width // 2), F32)
    places = pltpu.VMEM((blocks, 1, 128), F32)
    waves = [jax.ShapeDtypeStruct(pressure.shape, F32)] * 2
    cells = [jax.ShapeDtypeStruct(tile, F32)]
    parts = pl.pallas_call(
        functools.partial(kernel, capacity, slots, width),
        out_shape=[wave] * 2 + [cell] * 4 + [cell_z, cell_x],
        in_specs=[hbm] * 12,
        out_specs=[vmem] * 8,
        scratch_shapes=[wave] * 5 + [cell] * 2 + [
            pltpu.VMEM(tile, jnp.int32), table, table,
            pltpu.SMEM((kinds,), F32), pltpu.SMEM((kinds,), F32), dma((32,)),
            wave_z, wave_x, wave_x, wave_x, wave_x, wave_x, cell_z, cell_x,
            wave_z, wave_x, wave_z, wave_x, cell_z, cell_x, cell_z, cell_x, cell_z, cell_x,
            cell, pltpu.VMEM((planes // 2 * rows + 2 * planes, lateral), F32), wave_x,
            lines, lines, places, places,
            dma((12 * chunks + 8,)), dma((12 * chunks + 8,)), dma((chunks,)), dma((chunks,)), dma((1,)), dma((1,))],
        compiler_params=pltpu.CompilerParams(
            collective_id=0, has_side_effects=True, vmem_limit_bytes=58 * 1024 * 1024),
    )(pressure, pressure_prev, courant, nonlinearity, absorption, own_map.T, slot_table.T,
      displacement, displacement_prev, layer_labels, shear_table, viscosity_table)
    return pl.pallas_call(
        finish,
        out_shape=waves + cells * 3,
        in_specs=[vmem] * 8,
        out_specs=[hbm] * 5,
        scratch_shapes=[cell, dma((5,))],
        compiler_params=pltpu.CompilerParams(vmem_limit_bytes=40 * 1024 * 1024),
    )(*parts)


def solution(mesh):
    field = P(("group", "gx"), "gy", None)
    table = P(("group", "gx"), "gy")
    return jax.shard_map(
        local,
        mesh=mesh,
        in_specs=(field,) * 5 + (table,) * 2 + (field,) * 3 + (P("group"),) * 2,
        out_specs=(field,) * 5,
        check_vma=False,
    )
```

time: 31.1 us -> 25 us (0.80)
  Pallas kernels: 30.3 us -> 24.2 us
    pallas_call x1, Pallas kernels: 27.8 us -> 22 us  [local(): pl.pallas_call(functools.partial(kernel, capacity, slots, width), out_sha...]
where the time goes in v1:
time: 25 us; the launch traced here: 24.8 us
  Pallas kernels  24.2 us (97%)
  between operations  0.64 us (3%)
    pallas_call x1, Pallas kernels, local(): pl.pallas_call(functools.partial(kernel, capacity, slots, width), out_sha...  22 us
    pallas_call x1, Pallas kernels, local(): pl.pallas_call(finish, out_shape=waves + cells * 3, in_specs=[vmem] * 8,...  2.22 us

profile of v1, /device:TPU:0, one launch (start us, length us, event | category | flops | bytes accessed | tf_op | source)
XLA Modules:
  0.0 24.8 jit_solution(8094888713538262154)
XLA Ops:
  0.6 22.0 %shard_map.155 = (f32[24,16,768]{2,1,0:T(8,128)S(1)}, f32[24,16,768]{2,1,0:T(8,128)S(1)}, f32[16,32,384]{2,1,0:T(8,128)S(1)}, f32[16,32,384]{2,1,0:T(8,128)S(1)}...) custom-call(f32[24,16,768]{2,1,0:T(8,128)} %p_in.1, ...), custom_call_target="tpu_custom_call" | custom-call | tf_op jit(solution)/shard_map/pallas_call | solution.py:499
  22.6 2.2 %shard_map.156 = (f32[24,16,768]{2,1,0:T(8,128)}, f32[24,16,768]{2,1,0:T(8,128)}, f32[16,32,384]{2,1,0:T(8,128)}, f32[16,32,384]{2,1,0:T(8,128)}, f32[16,32,384]{2,1,0:T(8,128)}) custom-call(f32[24,16,768]{2,1,0:T(8,128)S(1)} %get-tuple-element.13.pm, f32[24,16,768]{2,1,0:T(8,128)S(1)} %get-tuple-element.14.pn, f32[16,32,384]{2,1,0:T(8,128)S(1)} %get-tuple-element.15.tf, ...), custom_call_target="tpu_custom_call" | custom-call | tf_op jit(solution)/shard_map/pallas_call | solution.py:516

commit v2 on v1

v2 whole, which is shorter than its diff:
```python
import functools

import jax
import jax.numpy as jnp
from jax import lax
from jax.experimental import pallas as pl
from jax.experimental.pallas import tpu as pltpu
from jax.sharding import PartitionSpec as P

MESH = pl.DeviceIdType.MESH
F32 = jnp.float32
BF16 = jnp.bfloat16


def iota(shape, dim):
    return lax.broadcasted_iota(jnp.int32, shape, dim)


def split(x):
    high = x.astype(BF16)
    low = (x - high.astype(F32)).astype(BF16)
    return high, low


def dot(a, b):
    return jnp.dot(a, b, preferred_element_type=F32)


def laplace(centre, up, down, left=0.0, right=0.0):
    rows, lanes = centre.shape
    row, lane = iota(centre.shape, 0), iota(centre.shape, 1)
    xm = jnp.where(row == 0, left, pltpu.roll(centre, 1, 0))
    xp = jnp.where(row == rows - 1, right, pltpu.roll(centre, rows - 1, 0))
    ym = jnp.where(lane == 0, 0.0, pltpu.roll(centre, 1, 1))
    yp = jnp.where(lane == lanes - 1, 0.0, pltpu.roll(centre, lanes - 1, 1))
    if up is None:
        beside = down
    elif down is None:
        beside = up
    else:
        beside = up + down
    return (beside + (xm + xp)) + ((ym + yp) - 6.0 * centre)


class Faces:
    def __init__(self, line, pieces, halo, recv, base):
        self.line, self.halo = line, halo
        self.up, self.down, self.one, self.two = [], [], [], []
        for i, (first, last, part) in enumerate(pieces):
            arrived = recv.at[base + i]
            self.up.append(line.copy(last, part(halo, 0), arrived, True))
            self.down.append(line.copy(first, part(halo, 1), arrived, False))
            self.one.append(line.copy(part(halo, 0), part(halo, 0), arrived, True))
            self.two.append(line.copy(part(halo, slice(None)), part(halo, slice(None)), arrived, True))

    def clear(self):
        @pl.when(jnp.logical_not(self.line.has_prev))
        def _():
            self.halo[0] = jnp.zeros(self.halo.shape[1:], F32)

        @pl.when(jnp.logical_not(self.line.has_next))
        def _():
            self.halo[1] = jnp.zeros(self.halo.shape[1:], F32)

    def start(self, i=0):
        pl.when(self.line.has_next)(self.up[i].start)
        pl.when(self.line.has_prev)(self.down[i].start)

    def wait(self, i=0):
        pl.when(self.line.inside)(self.two[i].wait_recv)
        pl.when(self.line.at_end)(self.one[i].wait_recv)


class Line:
    def __init__(self, axis, sent, token):
        size, self.index = lax.axis_size(axis), lax.axis_index(axis)
        index = self.index
        self.size, self.axis, self.sent, self.token = size, axis, sent, token
        self.next = jnp.where(index == size - 1, 0, index + 1)
        self.prev = jnp.where(index == 0, size - 1, index - 1)
        self.has_next, self.has_prev = index < size - 1, index > 0
        self.inside = self.has_next & self.has_prev
        self.at_end = (index == 0) | (index == size - 1)
        self.low = index < size // 2
        self.neighbours = jnp.where(index < size - 1, 1, 0) + jnp.where(index > 0, 1, 0)

    def copy(self, source, target, arrived, up):
        return pltpu.make_async_remote_copy(
            src_ref=source, dst_ref=target, send_sem=self.sent.at[0 if up else 1], recv_sem=arrived,
            device_id={self.axis: self.next if up else self.prev}, device_id_type=MESH)

    def greet(self, barrier):
        for here, other in ((self.has_next, self.next), (self.has_prev, self.prev)):
            @pl.when(here)
            def _():
                pl.semaphore_signal(barrier, inc=1, device_id={self.axis: other}, device_id_type=MESH)

    def tell_next(self):
        pl.semaphore_signal(self.token.at[0], inc=1, device_id={self.axis: self.next}, device_id_type=MESH)

    def tell_prev(self):
        pl.semaphore_signal(self.token.at[1], inc=1, device_id={self.axis: self.prev}, device_id_type=MESH)

    def open(self):
        pl.when(self.index == 0)(self.tell_next)
        pl.when(self.index == self.size - 1)(self.tell_prev)

    def pass_up(self, where):
        @pl.when(where & self.inside)
        def _():
            pl.semaphore_wait(self.token.at[0], 1)
            self.tell_next()

    def pass_down(self, where):
        @pl.when(where & self.inside)
        def _():
            pl.semaphore_wait(self.token.at[1], 1)
            self.tell_prev()

    def near(self):
        self.pass_up(self.low)
        self.pass_down(jnp.logical_not(self.low))

    def far(self):
        self.pass_up(jnp.logical_not(self.low))
        self.pass_down(self.low)

    def close(self):
        @pl.when(self.index == 0)
        def _():
            pl.semaphore_wait(self.token.at[1], 1)

        @pl.when(self.index == self.size - 1)
        def _():
            pl.semaphore_wait(self.token.at[0], 1)

    def wait_sent(self, ref, size):
        whole = ref.at[0:size]
        pl.when(self.has_next)(self.copy(whole, whole, self.sent.at[0], True).wait_send)
        pl.when(self.has_prev)(self.copy(whole, whole, self.sent.at[0], False).wait_send)


def kernel(
    capacity, slots, width,
    p_in, q_in, c_in, n_in, a_in, own_in, slot_in, u_in, w_in, k_in, shear_in, viscosity_in,
    pm, pn, tf, um, un, both, hz_out, hx_out,
    fields, now_before, k, tables, layers, load,
    faces_p, sides, fx_m, fx_n, fz_e, fx_e,
    hz_p, hx_p, hz_m, hx_m, hz_uw, hx_uw, hz_e, hx_e,
    rest, paired, gain, packed, got,
    sent_z, sent_x, recv, line_send, line_recv, token_z, token_x,
):
    _, planes, rows, lateral = fields.shape
    _, tile_rows, tile_cols, tile_depth = now_before.shape
    kinds = layers.shape[1]
    p, q, c, n, a = (fields.at[i] for i in range(5))
    u, w = now_before.at[0], now_before.at[1]
    own, slot = tables.at[0], tables.at[1]
    fx_p = [faces_p.at[i * planes:(i + 1) * planes] for i in range(2)]
    fz_p = [faces_p.at[2 * planes + i * rows:2 * planes + (i + 1) * rows] for i in range(2)]
    fx_c, fx_a = sides.at[0:2], sides.at[2:4]
    half = width // 2
    chunks = lateral // width
    gx, gy = lax.axis_size("gx"), lax.axis_size("gy")
    blocks = gx * gy
    me_x, me_y = lax.axis_index("gx"), lax.axis_index("gy")
    me = me_x * gy + me_y
    along_gx, along_gy = Line("gx", sent_z, token_z), Line("gy", sent_x, token_x)

    barrier = pltpu.get_barrier_semaphore()
    cuts = 3 if planes % 3 == 0 else 1
    step = planes // cuts

    def loads(at, total, pairs):
        copies = [pltpu.make_async_copy(s, d, load.at[at]) for s, d in pairs]
        return copies, pltpu.make_async_copy(total, total, load.at[at])

    def start(group):
        for copy in group[0]:
            copy.start()

    faces_in = loads(0, faces_p, (
        (p_in.at[:, 0, :], fx_p[0]), (p_in.at[:, rows - 1, :], fx_p[1]),
        (p_in.at[0], fz_p[0]), (p_in.at[planes - 1], fz_p[1])))
    waves_in = []
    for i in range(cuts):
        part = pl.ds(i * step, step)
        waves_in.append(loads(6 + i, fields.at[:, part], [
            (s.at[part], fields.at[j, part]) for j, s in enumerate((p_in, q_in, c_in, n_in, a_in))]))
    tables_in = loads(1, tables, ((own_in, own), (slot_in, slot)))
    sides_in = loads(2, sides, (
        (c_in.at[:, 0, :], sides.at[0]), (c_in.at[:, rows - 1, :], sides.at[1]),
        (a_in.at[:, 0, :], sides.at[2]), (a_in.at[:, rows - 1, :], sides.at[3])))
    cells_in = loads(3, now_before, ((u_in, u), (w_in, w)))
    kinds_in = loads(4, k, ((k_in, k),))
    layers_in = loads(5, layers, ((shear_in, layers.at[0]), (viscosity_in, layers.at[1])))

    along_gx.greet(barrier)
    along_gy.greet(barrier)
    for group in [faces_in] + waves_in + [sides_in, tables_in, cells_in, kinds_in, layers_in]:
        start(group)

    def lanes(i):
        return slice(i * width, (i + 1) * width)

    def depths(i):
        return slice(i * half, (i + 1) * half)

    def cut_all(first, last, at):
        def part(where):
            return lambda halo, side: halo.at[side, :, where]
        return [(first.at[:, at(i)], last.at[:, at(i)], part(at(i))) for i in range(chunks)]

    def both_of(first, last):
        return [(f, l, lambda halo, side, i=i: halo.at[side, i]) for i, (f, l) in enumerate(zip(first, last))]

    p_z = Faces(along_gx, cut_all(*fz_p, lanes), hz_p, recv, 0)
    p_x = Faces(along_gy, cut_all(*fx_p, lanes), hx_p, recv, chunks)
    m_z = Faces(along_gx, cut_all(pm.at[0], pm.at[planes - 1], lanes), hz_m, recv, 2 * chunks)
    m_x = Faces(along_gy, cut_all(fx_m.at[0], fx_m.at[1], lanes), hx_m, recv, 3 * chunks)
    e_z = Faces(along_gx, cut_all(fz_e.at[0], fz_e.at[1], depths), hz_e, recv, 4 * chunks)
    e_x = Faces(along_gy, cut_all(fx_e.at[0], fx_e.at[1], depths), hx_e, recv, 5 * chunks)
    uw_z = Faces(along_gx, both_of(
        (u_in.at[0], w_in.at[0]), (u_in.at[tile_rows - 1], w_in.at[tile_rows - 1])), hz_uw, recv, 6 * chunks)
    uw_x = Faces(along_gy, both_of(
        (u_in.at[:, 0, :], w_in.at[:, 0, :]),
        (u_in.at[:, tile_cols - 1, :], w_in.at[:, tile_cols - 1, :])), hx_uw, recv, 6 * chunks + 2)

    faces_in[1].wait()
    pl.semaphore_wait(barrier, along_gx.neighbours + along_gy.neighbours)
    for i in range(chunks):
        p_x.start(i)
        p_z.start(i)
    for item in (uw_x, uw_z):
        item.start(0)
        item.start(1)
    along_gx.open()
    for item in (p_z, p_x, m_z, m_x, uw_z, uw_x, e_z, e_x):
        item.clear()

    def wave(now, before, lap, z):
        return (2.0 * now - before + c[z] * lap + n[z] * (now * now - before * before)
                - 0.1 * a[z] * (now - before))

    def first(z, up, down):
        now = p[z]
        mid = wave(now, q[z], laplace(now, up, down), z)
        pm[z] = mid
        fx_m[0, pl.ds(z, 1), :] = mid[:1]
        fx_m[1, pl.ds(z, 1), :] = mid[-1:]

    for i, group in enumerate(waves_in):
        group[1].wait()
        low, high = i * step - 1, (i + 1) * step - 1
        if i == 0:
            first(0, None, p[1])
            low = 1
        if i == cuts - 1:
            high = planes - 1
        lax.fori_loop(low, high, lambda z, carry: (first(z, p[z - 1], p[z + 1]), carry)[1], 0, unroll=2)
        if i == cuts - 1:
            first(planes - 1, p[planes - 2], None)
        if i == 0:
            along_gx.near()
        if i == min(1, cuts - 1):
            along_gx.far()
        if i == cuts - 1:
            along_gx.close()
            along_gy.open()
    sides_in[1].wait()

    for i in range(chunks):
        at = lanes(i)
        p_x.wait(i)
        p_z.wait(i)
        top = c[0, :, at] * hz_p[0, :, at]
        bottom = c[planes - 1, :, at] * hz_p[1, :, at]
        pm[0, :, at] = pm[0, :, at] + top
        pm[planes - 1, :, at] = pm[planes - 1, :, at] + bottom
        z = iota((planes, width), 0)
        for side, row in ((0, 0), (1, rows - 1)):
            extra = sides[side, :, at] * hx_p[side, :, at]
            extra = extra + jnp.where(z == 0, top[row:row + 1], 0.0)
            extra = extra + jnp.where(z == planes - 1, bottom[row:row + 1], 0.0)
            mid = fx_m[side, :, at] + extra
            fx_m[side, :, at] = mid
            pm[:, row, at] = mid
        m_x.start(i)
        m_z.start(i)
    along_gy.near()

    def second(z, up, down):
        now = pm[z]
        new = wave(now, p[z], laplace(now, up, down), z)
        pn[z] = new
        fx_n[0, pl.ds(z, 1), :] = new[:1]
        fx_n[1, pl.ds(z, 1), :] = new[-1:]
        return 0.1 * a[z] * (now * now + new * new) * lax.rsqrt(c[z])

    def pair_at(i):
        return pl.ds(pl.multiple_of(i * rows, rows), rows)

    paired[pair_at(0), :] = second(0, None, pm[1]) + second(1, pm[0], pm[2])
    last = planes // 2 - 1

    def two(i, carry):
        z = 2 * i
        paired[pair_at(i), :] = second(z, pm[z - 1], pm[z + 1]) + second(z + 1, pm[z], pm[z + 2])
        return carry

    middle = last // 2 + 1
    lax.fori_loop(1, middle, two, 0)
    along_gy.far()
    lax.fori_loop(middle, last, two, 0)
    paired[pair_at(last), :] = second(planes - 2, pm[planes - 3], pm[planes - 1]) + second(
        planes - 1, pm[planes - 2], None)
    gain[...] = 0.1 * sides[2:4] * lax.rsqrt(sides[0:2])

    tables_in[1].wait()
    lines_x, lines_z = own.shape
    count = lines_z * rows
    total = count + 2 * planes
    padded = -(-total // 128) * 128

    def line_of(column):
        beyond = column - count
        side = jnp.where(beyond >= planes, 1, 0)
        x = jnp.where(column < count, lax.rem(column, rows) // 2, side * (lines_x - 1))
        z = jnp.where(column < count, column // rows, (beyond - side * planes) // 2)
        return z, x

    def along_lanes(table):
        z_of, x_of = line_of(iota((lines_x, padded), 1))
        here = x_of == iota((lines_x, padded), 0)
        result = jnp.zeros((lines_x, padded), F32)
        for z in range(lines_z):
            result = result + jnp.where(here & (z_of == z), table[:, z:z + 1], 0.0)
        return jnp.sum(result, axis=0, keepdims=True)

    owners = own[...].astype(F32)
    owner_lane = along_lanes(owners)
    owner_row = jnp.transpose(jnp.broadcast_to(owner_lane, (128, padded)))[:count, :1]
    owner_lane = owner_lane[:, :total]
    place_lane = along_lanes(slot[...].astype(F32))[:, :total]
    z_of, x_of = line_of(iota((count, total), 1))
    earlier = iota((count, total), 0) // 2 < z_of * lines_x + x_of
    rank = 0.5 * jnp.sum(
        jnp.where((owner_row == owner_lane) & earlier, 1.0, 0.0), axis=0, keepdims=True)
    target = owner_lane * float(slots) + rank
    match = iota((blocks * slots, total), 0).astype(F32) == target
    column = iota((blocks * slots, total), 1)
    counted = (lax.rem(column, 2) == 0) & (column < count)
    places = jnp.sum(jnp.where(match & counted, place_lane + 1.0, 0.0), axis=1, keepdims=True)
    aligned = lax.rem(iota((blocks * slots, 128), 0), slots) == lax.rem(iota((blocks * slots, 128), 1), slots)
    places = jnp.where(aligned, places, 0.0).reshape(blocks, slots, 128)
    places = jnp.sum(places, axis=1, keepdims=True)
    match = jnp.where(match, 1.0, 0.0).astype(BF16)

    used = [pl.ds(0, capacity + 1)] + [pl.ds(0, capacity)] * (chunks - 1)
    others = pl.ds(0, blocks - 1)

    def line_copy(i, source, target_ref, x, y):
        return pltpu.make_async_remote_copy(
            src_ref=source, dst_ref=target_ref, send_sem=line_send.at[i], recv_sem=line_recv.at[i],
            device_id={"gx": x, "gy": y}, device_id_type=MESH)

    def turn(index, by, size):
        moved = index + by
        return jnp.where(moved >= size, moved - size, moved)

    far_first = sorted(range(gy), key=lambda by: -min(by, gy - by))
    xs, ys = [turn(me_x, by, gx) for by in range(gx)], [turn(me_y, by, gy) for by in range(gy)]

    def start_lines(i):
        def send(x, y):
            other = x * gy + y
            line_copy(i, packed.at[i, other, used[i]], got.at[i, me, used[i]], x, y).start()

        if blocks <= 32:
            for by in far_first:
                for ax in range(gx):
                    if by or ax:
                        send(xs[ax], ys[by])
        else:
            def one(d, carry):
                other = lax.rem(me + d, blocks)
                send(other // gy, lax.rem(other, gy))
                return carry

            lax.fori_loop(1, blocks, one, 0)
        got[i, me] = packed[i, me]

    all_lines = [line_copy(
        i, packed.at[i, others, used[i]], got.at[i, others, used[i]], me_x, me_y) for i in range(chunks)]

    lanes_two = jnp.where(iota((width, half), 0) // 2 == iota((width, half), 1), 0.125, 0.0).astype(BF16)
    for i in range(chunks):
        at = lanes(i)
        m_x.wait(i)
        m_z.wait(i)
        for side, z, pair in ((0, 0, 0), (1, planes - 1, last)):
            old = pn[z, :, at]
            extra = c[z, :, at] * hz_m[side, :, at]
            new = old + extra
            pn[z, :, at] = new
            fx_n[0, z:z + 1, at] = new[:1]
            fx_n[1, z:z + 1, at] = new[-1:]
            where = slice(pair * rows, (pair + 1) * rows)
            paired[where, at] = paired[where, at] + (
                0.1 * a[z, :, at] * lax.rsqrt(c[z, :, at]) * (extra * (2.0 * old + extra)))
        for side in range(2):
            old = fx_n[side, :, at]
            extra = sides[side, :, at] * hx_m[side, :, at]
            fx_n[side, :, at] = old + extra
            paired[count + side * planes:count + (side + 1) * planes, at] = (
                gain[side, :, at] * (extra * (2.0 * old + extra)))
        high, low = split(paired[:, at])
        coarse = dot(high, lanes_two) + dot(low, lanes_two)
        high, low = split(coarse)
        coarse = (dot(match, high) + dot(match, low)).reshape(blocks, slots, half)
        if i == 0:
            coarse = jnp.where(iota(coarse.shape, 1) == capacity, places, coarse)
            along_gy.close()
        packed[i] = coarse
        start_lines(i)

    for side, row in ((0, 0), (1, rows - 1)):
        pn[:, row, :] = fx_n[side]

    for group in (cells_in, kinds_in, layers_in):
        group[1].wait()
    for item in (uw_z, uw_x):
        item.wait(0)
        item.wait(1)

    def elastic(z, u_up, u_down, w_up, w_down):
        now, before, kind = u[z], w[z], k[z]
        lap_u = laplace(now, u_up, u_down, hx_uw[0, 0, pl.ds(z, 1), :], hx_uw[1, 0, pl.ds(z, 1), :])
        lap_w = laplace(before, w_up, w_down, hx_uw[0, 1, pl.ds(z, 1), :], hx_uw[1, 1, pl.ds(z, 1), :])
        shear, viscosity = jnp.zeros(now.shape, F32), jnp.zeros(now.shape, F32)
        for i in range(kinds):
            shear = jnp.where(kind == i, layers[0, i], shear)
            viscosity = jnp.where(kind == i, layers[1, i], viscosity)
        mid = 2.0 * now - before + shear * lap_u + viscosity * (lap_u - lap_w)
        um[z] = mid
        fx_e[0, pl.ds(z, 1), :] = mid[:1]
        fx_e[1, pl.ds(z, 1), :] = mid[-1:]
        rest[z] = now + viscosity * lap_u
        both[z] = shear + viscosity

    elastic(0, hz_uw[0, 0], u[1], hz_uw[0, 1], w[1])
    elastic(tile_rows - 1, u[tile_rows - 2], hz_uw[1, 0], w[tile_rows - 2], hz_uw[1, 1])
    lax.fori_loop(1, tile_rows - 1, lambda z, carry: (
        elastic(z, u[z - 1], u[z + 1], w[z - 1], w[z + 1]), carry)[1], 0)

    cells = tile_rows * tile_cols

    def landings():
        spread = -(-blocks * slots // 128)
        sources = jnp.concatenate([got[0, :, capacity, :]] * spread, axis=1)[:, :blocks * slots]
        mine = iota((blocks, blocks * slots), 1) // slots == iota((blocks, blocks * slots), 0)
        spots = jnp.sum(jnp.where(mine, sources, 0.0), axis=0, keepdims=True) - 1.0

        def landing_of(cell):
            return jnp.where(cell.astype(F32) == spots, 1.0, 0.0).astype(BF16)

        landing = landing_of(iota((cells, blocks * slots), 0))
        edges = 2 * tile_cols + 2 * tile_rows
        edge = iota((edges, blocks * slots), 0)
        beyond = edge - 2 * tile_cols
        edge_landing = landing_of(jnp.where(
            edge < tile_cols, edge, jnp.where(
                edge < 2 * tile_cols, edge + (cells - 2 * tile_cols), jnp.where(
                    beyond < tile_rows, beyond * tile_cols, (beyond - tile_rows) * tile_cols + tile_cols - 1))))
        real = lax.rem(iota((blocks * slots, half), 0), slots) < capacity
        return landing, edge_landing, real

    chunk = 4 if tile_rows % 4 == 0 else 1
    for i in range(chunks):
        at = depths(i)
        all_lines[i].wait_recv()
        if i == 0:
            landing, edge_landing, real = landings()
        lines = jnp.where(real, got[i].reshape(blocks * slots, half), 0.0)
        parts = jnp.concatenate(split(lines), axis=1)

        def sums(where):
            result = dot(where, parts)
            return result[:, :half] + result[:, half:]

        edge_force = 0.25 * sums(edge_landing)
        for side, z in ((0, 0), (1, tile_rows - 1)):
            fz_e[side, :, at] = um[z, :, at] + edge_force[side * tile_cols:(side + 1) * tile_cols]
            here = 2 * tile_cols + side * tile_rows
            fx_e[side, :, at] = fx_e[side, :, at] + edge_force[here:here + tile_rows]
        e_x.start(i)
        e_z.start(i)
        for r in range(0, tile_rows, chunk):
            force = sums(landing[r * tile_cols:(r + chunk) * tile_cols]).reshape(chunk, tile_cols, half)
            tf[r:r + chunk, :, at] = force
            um[r:r + chunk, :, at] = um[r:r + chunk, :, at] + 0.25 * force

    def final(z, up, down):
        now = um[z]
        un[z] = 2.0 * now - rest[z] + both[z] * laplace(now, up, down) + 0.25 * tf[z]

    final(0, None, um[1])
    final(tile_rows - 1, um[tile_rows - 2], None)
    lax.fori_loop(1, tile_rows - 1, lambda z, carry: (final(z, um[z - 1], um[z + 1]), carry)[1], 0, unroll=2)

    for item in all_lines:
        item.wait_send()
    for i in range(chunks):
        e_z.wait(i)
        e_x.wait(i)
    hz_out[...] = hz_e[...]
    hx_out[...] = hx_e[...]
    along_gx.wait_sent(paired, 2 * rows + 3 * tile_cols * tile_depth // lateral)
    along_gy.wait_sent(paired, 2 * planes + 3 * tile_rows * tile_depth // lateral)


def finish(pm, pn, tf, um, partial, both, hz, hx, pm_out, pn_out, tf_out, um_out, un_out, un, sems):
    copies = [pltpu.make_async_copy(s, d, sems.at[i]) for i, (s, d) in enumerate(
        ((pm, pm_out), (pn, pn_out), (tf, tf_out), (um, um_out)))]
    for copy in copies:
        copy.start()
    tile_rows, tile_cols, _ = um.shape

    def final(z, carry):
        scale = both[z]
        row = iota(scale.shape, 0)
        extra = jnp.where(row == 0, hx[0, pl.ds(z, 1), :], 0.0) + jnp.where(
            row == tile_cols - 1, hx[1, pl.ds(z, 1), :], 0.0)
        un[z] = partial[z] + scale * extra
        return carry

    lax.fori_loop(0, tile_rows, final, 0)
    for side, z in ((0, 0), (1, tile_rows - 1)):
        un[z] = un[z] + both[z] * hz[side]
    copies.append(pltpu.make_async_copy(un, un_out, sems.at[4]))
    copies[4].start()
    for copy in copies:
        copy.wait()


def local(pressure, pressure_prev, courant, nonlinearity, absorption, own_map, slot_table,
          displacement, displacement_prev, layer_labels, shear_table, viscosity_table):
    planes, rows, lateral = pressure.shape
    tile = displacement.shape
    blocks = lax.axis_size("gx") * lax.axis_size("gy")
    capacity = max(2, own_map.shape[0] * own_map.shape[1] // blocks)
    slots = -(-(capacity + 1) // 8) * 8
    width = 256
    chunks = lateral // width
    hbm = pl.BlockSpec(memory_space=pltpu.HBM)
    vmem = pl.BlockSpec(memory_space=pltpu.VMEM)
    wave, cell = pltpu.VMEM(pressure.shape, F32), pltpu.VMEM(tile, F32)

    def along_z(shape):
        return pltpu.VMEM((2,) + shape[1:], F32)

    def along_x(shape):
        return pltpu.VMEM((2, shape[0], shape[2]), F32)

    dma, regular = pltpu.SemaphoreType.DMA, pltpu.SemaphoreType.REGULAR
    kinds = shear_table.shape[0]
    wave_z, wave_x, cell_z, cell_x = along_z(pressure.shape), along_x(pressure.shape), along_z(tile), along_x(tile)
    lines = pltpu.VMEM((chunks, blocks, slots, width // 2), F32)
    waves = [jax.ShapeDtypeStruct(pressure.shape, F32)] * 2
    cells = [jax.ShapeDtypeStruct(tile, F32)]
    parts = pl.pallas_call(
        functools.partial(kernel, capacity, slots, width),
        out_shape=[wave] * 2 + [cell] * 4 + [cell_z, cell_x],
        in_specs=[hbm] * 12,
        out_specs=[vmem] * 8,
        scratch_shapes=[
            pltpu.VMEM((5,) + pressure.shape, F32), pltpu.VMEM((2,) + tile, F32), pltpu.VMEM(tile, jnp.int32),
            pltpu.VMEM((2,) + own_map.shape[::-1], jnp.int32), pltpu.SMEM((2, kinds), F32), dma((9,)),
            pltpu.VMEM((2 * (planes + rows), lateral), F32), pltpu.VMEM((4, planes, lateral), F32),
            wave_x, wave_x, cell_z, cell_x,
            wave_z, wave_x, wave_z, wave_x,
            pltpu.VMEM((2, 2) + tile[1:], F32), pltpu.VMEM((2, 2, tile[0], tile[2]), F32), cell_z, cell_x,
            cell, pltpu.VMEM((planes // 2 * rows + 2 * planes, lateral), F32), wave_x, lines, lines,
            dma((2,)), dma((2,)), dma((6 * chunks + 4,)), dma((chunks,)), dma((chunks,)), regular((2,)), regular((2,))],
        compiler_params=pltpu.CompilerParams(
            collective_id=0, has_side_effects=True, vmem_limit_bytes=58 * 1024 * 1024),
    )(pressure, pressure_prev, courant, nonlinearity, absorption, own_map.T, slot_table.T,
      displacement, displacement_prev, layer_labels, shear_table, viscosity_table)
    return pl.pallas_call(
        finish,
        out_shape=waves + cells * 3,
        in_specs=[vmem] * 8,
        out_specs=[hbm] * 5,
        scratch_shapes=[cell, dma((5,))],
        compiler_params=pltpu.CompilerParams(vmem_limit_bytes=40 * 1024 * 1024),
    )(*parts)


def solution(mesh):
    field = P(("group", "gx"), "gy", None)
    table = P(("group", "gx"), "gy")
    return jax.shard_map(
        local,
        mesh=mesh,
        in_specs=(field,) * 5 + (table,) * 2 + (field,) * 3 + (P("group"),) * 2,
        out_specs=(field,) * 5,
        check_vma=False,
    )
```

time: 25 us -> 22.8 us (0.912)
  Pallas kernels: 24.2 us -> 21.8 us
    pallas_call x1, Pallas kernels: 22 us -> 19.6 us  [local(): pl.pallas_call(functools.partial(kernel, capacity, slots, width), out_sha...]
where the time goes in v2:
time: 22.8 us; the launch traced here: 22.5 us
  Pallas kernels  21.8 us (96%)
  between operations  0.64 us (3%)
    pallas_call x1, Pallas kernels, local(): pl.pallas_call(functools.partial(kernel, capacity, slots, width), out_sha...  19.6 us
    pallas_call x1, Pallas kernels, local(): pl.pallas_call(finish, out_shape=waves + cells * 3, in_specs=[vmem] * 8,...  2.22 us

profile of v2, /device:TPU:0, one launch (start us, length us, event | category | flops | bytes accessed | tf_op | source)
XLA Modules:
  0.0 22.5 jit_solution(11035713837828969927)
XLA Ops:
  0.6 19.6 %shard_map.155 = (f32[24,16,768]{2,1,0:T(8,128)S(1)}, f32[24,16,768]{2,1,0:T(8,128)S(1)}, f32[16,32,384]{2,1,0:T(8,128)S(1)}, f32[16,32,384]{2,1,0:T(8,128)S(1)}...) custom-call(f32[24,16,768]{2,1,0:T(8,128)} %p_in.1, ...), custom_call_target="tpu_custom_call" | custom-call | tf_op jit(solution)/shard_map/pallas_call | solution.py:571
  20.2 2.2 %shard_map.156 = (f32[24,16,768]{2,1,0:T(8,128)}, f32[24,16,768]{2,1,0:T(8,128)}, f32[16,32,384]{2,1,0:T(8,128)}, f32[16,32,384]{2,1,0:T(8,128)}, f32[16,32,384]{2,1,0:T(8,128)}) custom-call(f32[24,16,768]{2,1,0:T(8,128)S(1)} %get-tuple-element.13.pm, f32[24,16,768]{2,1,0:T(8,128)S(1)} %get-tuple-element.14.pn, f32[16,32,384]{2,1,0:T(8,128)S(1)} %get-tuple-element.15.tf, ...), custom_call_target="tpu_custom_call" | custom-call | tf_op jit(solution)/shard_map/pallas_call | solution.py:589

commit v3 on v2

--- a/solution.py
+++ b/solution.py
@@ -43,13 +43,16 @@
 
 
 class Faces:
-    def __init__(self, line, pieces, halo, recv, base):
+    def __init__(self, line, pieces, halo, recv, base, together=False):
         self.line, self.halo = line, halo
         self.up, self.down, self.one, self.two = [], [], [], []
         for i, (first, last, part) in enumerate(pieces):
-            arrived = recv.at[base + i]
+            arrived = recv.at[base if together else base + i]
             self.up.append(line.copy(last, part(halo, 0), arrived, True))
             self.down.append(line.copy(first, part(halo, 1), arrived, False))
+        parts = [lambda halo, side: halo.at[side]] if together else [part for _, _, part in pieces]
+        for i, part in enumerate(parts):
+            arrived = recv.at[base + i]
             self.one.append(line.copy(part(halo, 0), part(halo, 0), arrived, True))
             self.two.append(line.copy(part(halo, slice(None)), part(halo, slice(None)), arrived, True))
 
@@ -218,22 +221,20 @@
     p_x = Faces(along_gy, cut_all(*fx_p, lanes), hx_p, recv, chunks)
     m_z = Faces(along_gx, cut_all(pm.at[0], pm.at[planes - 1], lanes), hz_m, recv, 2 * chunks)
     m_x = Faces(along_gy, cut_all(fx_m.at[0], fx_m.at[1], lanes), hx_m, recv, 3 * chunks)
-    e_z = Faces(along_gx, cut_all(fz_e.at[0], fz_e.at[1], depths), hz_e, recv, 4 * chunks)
-    e_x = Faces(along_gy, cut_all(fx_e.at[0], fx_e.at[1], depths), hx_e, recv, 5 * chunks)
+    at = 4 * chunks
+    e_z = Faces(along_gx, cut_all(fz_e.at[0], fz_e.at[1], depths), hz_e, recv, at, True)
+    e_x = Faces(along_gy, cut_all(fx_e.at[0], fx_e.at[1], depths), hx_e, recv, at + 1, True)
     uw_z = Faces(along_gx, both_of(
-        (u_in.at[0], w_in.at[0]), (u_in.at[tile_rows - 1], w_in.at[tile_rows - 1])), hz_uw, recv, 6 * chunks)
+        (u_in.at[0], w_in.at[0]), (u_in.at[tile_rows - 1], w_in.at[tile_rows - 1])), hz_uw, recv, at + 2, True)
     uw_x = Faces(along_gy, both_of(
         (u_in.at[:, 0, :], w_in.at[:, 0, :]),
-        (u_in.at[:, tile_cols - 1, :], w_in.at[:, tile_cols - 1, :])), hx_uw, recv, 6 * chunks + 2)
+        (u_in.at[:, tile_cols - 1, :], w_in.at[:, tile_cols - 1, :])), hx_uw, recv, at + 3, True)
 
     faces_in[1].wait()
     pl.semaphore_wait(barrier, along_gx.neighbours + along_gy.neighbours)
     for i in range(chunks):
         p_x.start(i)
         p_z.start(i)
-    for item in (uw_x, uw_z):
-        item.start(0)
-        item.start(1)
     along_gx.open()
     for item in (p_z, p_x, m_z, m_x, uw_z, uw_x, e_z, e_x):
         item.clear()
@@ -269,6 +270,46 @@
             along_gy.open()
     sides_in[1].wait()
 
+    tables_in[1].wait()
+    lines_x, lines_z = own.shape
+    count = lines_z * rows
+    total = count + 2 * planes
+    padded = -(-total // 128) * 128
+
+    def line_of(column):
+        beyond = column - count
+        side = jnp.where(beyond >= planes, 1, 0)
+        x = jnp.where(column < count, lax.rem(column, rows) // 2, side * (lines_x - 1))
+        z = jnp.where(column < count, column // rows, (beyond - side * planes) // 2)
+        return z, x
+
+    def along_lanes(table):
+        z_of, x_of = line_of(iota((lines_x, padded), 1))
+        here = x_of == iota((lines_x, padded), 0)
+        result = jnp.zeros((lines_x, padded), F32)
+        for z in range(lines_z):
+            result = result + jnp.where(here & (z_of == z), table[:, z:z + 1], 0.0)
+        return jnp.sum(result, axis=0, keepdims=True)
+
+    owners = own[...].astype(F32)
+    owner_lane = along_lanes(owners)
+    owner_row = jnp.transpose(jnp.broadcast_to(owner_lane, (128, padded)))[:count, :1]
+    owner_lane = owner_lane[:, :total]
+    place_lane = along_lanes(slot[...].astype(F32))[:, :total]
+    z_of, x_of = line_of(iota((count, total), 1))
+    earlier = iota((count, total), 0) // 2 < z_of * lines_x + x_of
+    rank = 0.5 * jnp.sum(
+        jnp.where((owner_row == owner_lane) & earlier, 1.0, 0.0), axis=0, keepdims=True)
+    target = owner_lane * float(slots) + rank
+    match = iota((blocks * slots, total), 0).astype(F32) == target
+    column = iota((blocks * slots, total), 1)
+    counted = (lax.rem(column, 2) == 0) & (column < count)
+    places = jnp.sum(jnp.where(match & counted, place_lane + 1.0, 0.0), axis=1, keepdims=True)
+    aligned = lax.rem(iota((blocks * slots, 128), 0), slots) == lax.rem(iota((blocks * slots, 128), 1), slots)
+    places = jnp.where(aligned, places, 0.0).reshape(blocks, slots, 128)
+    places = jnp.sum(places, axis=1, keepdims=True)
+    match = jnp.where(match, 1.0, 0.0).astype(BF16)
+
     for i in range(chunks):
         at = lanes(i)
         p_x.wait(i)
@@ -287,6 +328,9 @@
             pm[:, row, at] = mid
         m_x.start(i)
         m_z.start(i)
+    for item in (uw_x, uw_z):
+        item.start(0)
+        item.start(1)
     along_gy.near()
 
     def second(z, up, down):
@@ -315,46 +359,6 @@
     paired[pair_at(last), :] = second(planes - 2, pm[planes - 3], pm[planes - 1]) + second(
         planes - 1, pm[planes - 2], None)
     gain[...] = 0.1 * sides[2:4] * lax.rsqrt(sides[0:2])
-
-    tables_in[1].wait()
-    lines_x, lines_z = own.shape
-    count = lines_z * rows
-    total = count + 2 * planes
-    padded = -(-total // 128) * 128
-
-    def line_of(column):
-        beyond = column - count
-        side = jnp.where(beyond >= planes, 1, 0)
-        x = jnp.where(column < count, lax.rem(column, rows) // 2, side * (lines_x - 1))
-        z = jnp.where(column < count, column // rows, (beyond - side * planes) // 2)
-        return z, x
-
-    def along_lanes(table):
-        z_of, x_of = line_of(iota((lines_x, padded), 1))
-        here = x_of == iota((lines_x, padded), 0)
-        result = jnp.zeros((lines_x, padded), F32)
-        for z in range(lines_z):
-            result = result + jnp.where(here & (z_of == z), table[:, z:z + 1], 0.0)
-        return jnp.sum(result, axis=0, keepdims=True)
-
-    owners = own[...].astype(F32)
-    owner_lane = along_lanes(owners)
-    owner_row = jnp.transpose(jnp.broadcast_to(owner_lane, (128, padded)))[:count, :1]
-    owner_lane = owner_lane[:, :total]
-    place_lane = along_lanes(slot[...].astype(F32))[:, :total]
-    z_of, x_of = line_of(iota((count, total), 1))
-    earlier = iota((count, total), 0) // 2 < z_of * lines_x + x_of
-    rank = 0.5 * jnp.sum(
-        jnp.where((owner_row == owner_lane) & earlier, 1.0, 0.0), axis=0, keepdims=True)
-    target = owner_lane * float(slots) + rank
-    match = iota((blocks * slots, total), 0).astype(F32) == target
-    column = iota((blocks * slots, total), 1)
-    counted = (lax.rem(column, 2) == 0) & (column < count)
-    places = jnp.sum(jnp.where(match & counted, place_lane + 1.0, 0.0), axis=1, keepdims=True)
-    aligned = lax.rem(iota((blocks * slots, 128), 0), slots) == lax.rem(iota((blocks * slots, 128), 1), slots)
-    places = jnp.where(aligned, places, 0.0).reshape(blocks, slots, 128)
-    places = jnp.sum(places, axis=1, keepdims=True)
-    match = jnp.where(match, 1.0, 0.0).astype(BF16)
 
     used = [pl.ds(0, capacity + 1)] + [pl.ds(0, capacity)] * (chunks - 1)
     others = pl.ds(0, blocks - 1)
@@ -429,9 +433,8 @@
 
     for group in (cells_in, kinds_in, layers_in):
         group[1].wait()
-    for item in (uw_z, uw_x):
-        item.wait(0)
-        item.wait(1)
+    uw_z.wait()
+    uw_x.wait()
 
     def elastic(z, u_up, u_down, w_up, w_down):
         now, before, kind = u[z], w[z], k[z]
@@ -510,9 +513,8 @@
 
     for item in all_lines:
         item.wait_send()
-    for i in range(chunks):
-        e_z.wait(i)
-        e_x.wait(i)
+    e_z.wait()
+    e_x.wait()
     hz_out[...] = hz_e[...]
     hx_out[...] = hx_e[...]
     along_gx.wait_sent(paired, 2 * rows + 3 * tile_cols * tile_depth // lateral)
@@ -581,7 +583,7 @@
             wave_z, wave_x, wave_z, wave_x,
             pltpu.VMEM((2, 2) + tile[1:], F32), pltpu.VMEM((2, 2, tile[0], tile[2]), F32), cell_z, cell_x,
             cell, pltpu.VMEM((planes // 2 * rows + 2 * planes, lateral), F32), wave_x, lines, lines,
-            dma((2,)), dma((2,)), dma((6 * chunks + 4,)), dma((chunks,)), dma((chunks,)), regular((2,)), regular((2,))],
+            dma((2,)), dma((2,)), dma((4 * chunks + 4,)), dma((chunks,)), dma((chunks,)), regular((2,)), regular((2,))],
         compiler_params=pltpu.CompilerParams(
             collective_id=0, has_side_effects=True, vmem_limit_bytes=58 * 1024 * 1024),
     )(pressure, pressure_prev, courant, nonlinearity, absorption, own_map.T, slot_table.T,

time: 22.8 us -> 22.6 us (level)
    pallas_call x1, Pallas kernels: 19.6 us -> 19.4 us  [local(): pl.pallas_call(functools.partial(kernel, capacity, slots, width), out_sha...]
where the time goes in v3:
time: 22.6 us; the launch traced here: 22.2 us
  Pallas kernels  21.6 us (96%)
  between operations  0.64 us (3%)
    pallas_call x1, Pallas kernels, local(): pl.pallas_call(functools.partial(kernel, capacity, slots, width), out_sha...  19.4 us
    pallas_call x1, Pallas kernels, local(): pl.pallas_call(finish, out_shape=waves + cells * 3, in_specs=[vmem] * 8,...  2.22 us

profile of v3, /device:TPU:0, one launch (start us, length us, event | category | flops | bytes accessed | tf_op | source)
XLA Modules:
  0.0 22.2 jit_solution(12490835824158656855)
XLA Ops:
  0.6 19.4 %shard_map.155 = (f32[24,16,768]{2,1,0:T(8,128)S(1)}, f32[24,16,768]{2,1,0:T(8,128)S(1)}, f32[16,32,384]{2,1,0:T(8,128)S(1)}, f32[16,32,384]{2,1,0:T(8,128)S(1)}...) custom-call(f32[24,16,768]{2,1,0:T(8,128)} %p_in.1, ...), custom_call_target="tpu_custom_call" | custom-call | tf_op jit(solution)/shard_map/pallas_call | solution.py:573
  20.0 2.2 %shard_map.156 = (f32[24,16,768]{2,1,0:T(8,128)}, f32[24,16,768]{2,1,0:T(8,128)}, f32[16,32,384]{2,1,0:T(8,128)}, f32[16,32,384]{2,1,0:T(8,128)}, f32[16,32,384]{2,1,0:T(8,128)}) custom-call(f32[24,16,768]{2,1,0:T(8,128)S(1)} %get-tuple-element.13.pm, f32[24,16,768]{2,1,0:T(8,128)S(1)} %get-tuple-element.14.pn, f32[16,32,384]{2,1,0:T(8,128)S(1)} %get-tuple-element.15.tf, ...), custom_call_target="tpu_custom_call" | custom-call | tf_op jit(solution)/shard_map/pallas_call | solution.py:591

commit v4 on v3

--- a/solution.py
+++ b/solution.py
@@ -171,7 +171,7 @@
     along_gx, along_gy = Line("gx", sent_z, token_z), Line("gy", sent_x, token_x)
 
     barrier = pltpu.get_barrier_semaphore()
-    cuts = 3 if planes % 3 == 0 else 1
+    cuts = 6 if planes % 6 == 0 else 1
     step = planes // cuts
 
     def loads(at, total, pairs):
@@ -261,9 +261,9 @@
         lax.fori_loop(low, high, lambda z, carry: (first(z, p[z - 1], p[z + 1]), carry)[1], 0, unroll=2)
         if i == cuts - 1:
             first(planes - 1, p[planes - 2], None)
-        if i == 0:
+        if i == (cuts + 2) // 3 - 1:
             along_gx.near()
-        if i == min(1, cuts - 1):
+        if i == max(2 * cuts // 3 - 1, 0):
             along_gx.far()
         if i == cuts - 1:
             along_gx.close()
@@ -368,12 +368,14 @@
             src_ref=source, dst_ref=target_ref, send_sem=line_send.at[i], recv_sem=line_recv.at[i],
             device_id={"gx": x, "gy": y}, device_id_type=MESH)
 
-    def turn(index, by, size):
-        moved = index + by
-        return jnp.where(moved >= size, moved - size, moved)
-
-    far_first = sorted(range(gy), key=lambda by: -min(by, gy - by))
-    xs, ys = [turn(me_x, by, gx) for by in range(gx)], [turn(me_y, by, gy) for by in range(gy)]
+    def far_first(index, size):
+        def place(j):
+            down, low = size - 1 - j, index < size // 2
+            return jnp.where(low, jnp.where(down > index, down, down - 1), jnp.where(j < index, j, j + 1))
+
+        return [place(j) for j in range(size - 1)] + [index]
+
+    xs, ys = far_first(me_x, gx), far_first(me_y, gy)
 
     def start_lines(i):
         def send(x, y):
@@ -381,10 +383,10 @@
             line_copy(i, packed.at[i, other, used[i]], got.at[i, me, used[i]], x, y).start()
 
         if blocks <= 32:
-            for by in far_first:
-                for ax in range(gx):
-                    if by or ax:
-                        send(xs[ax], ys[by])
+            for y in ys:
+                for x in xs:
+                    if x is not me_x or y is not me_y:
+                        send(x, y)
         else:
             def one(d, carry):
                 other = lax.rem(me + d, blocks)
@@ -577,7 +579,7 @@
         out_specs=[vmem] * 8,
         scratch_shapes=[
             pltpu.VMEM((5,) + pressure.shape, F32), pltpu.VMEM((2,) + tile, F32), pltpu.VMEM(tile, jnp.int32),
-            pltpu.VMEM((2,) + own_map.shape[::-1], jnp.int32), pltpu.SMEM((2, kinds), F32), dma((9,)),
+            pltpu.VMEM((2,) + own_map.shape[::-1], jnp.int32), pltpu.SMEM((2, kinds), F32), dma((12,)),
             pltpu.VMEM((2 * (planes + rows), lateral), F32), pltpu.VMEM((4, planes, lateral), F32),
             wave_x, wave_x, cell_z, cell_x,
             wave_z, wave_x, wave_z, wave_x,

time: 22.6 us -> 22.5 us (level); the launches traced: 22.2 us -> 22.4 us
  no operation moved by 1% of the time
where the time goes in v4:
time: 22.5 us; the launch traced here: 22.4 us
  Pallas kernels  21.7 us (96%)
  between operations  0.64 us (3%)
    pallas_call x1, Pallas kernels, local(): pl.pallas_call(functools.partial(kernel, capacity, slots, width), out_sha...  19.5 us
    pallas_call x1, Pallas kernels, local(): pl.pallas_call(finish, out_shape=waves + cells * 3, in_specs=[vmem] * 8,...  2.22 us

profile of v4, /device:TPU:0, one launch (start us, length us, event | category | flops | bytes accessed | tf_op | source)
XLA Modules:
  0.0 22.4 jit_solution(10525256973525961749)
XLA Ops:
  0.6 19.5 %shard_map.155 = (f32[24,16,768]{2,1,0:T(8,128)S(1)}, f32[24,16,768]{2,1,0:T(8,128)S(1)}, f32[16,32,384]{2,1,0:T(8,128)S(1)}, f32[16,32,384]{2,1,0:T(8,128)S(1)}...) custom-call(f32[24,16,768]{2,1,0:T(8,128)} %p_in.1, ...), custom_call_target="tpu_custom_call" | custom-call | tf_op jit(solution)/shard_map/pallas_call | solution.py:575
  20.1 2.2 %shard_map.156 = (f32[24,16,768]{2,1,0:T(8,128)}, f32[24,16,768]{2,1,0:T(8,128)}, f32[16,32,384]{2,1,0:T(8,128)}, f32[16,32,384]{2,1,0:T(8,128)}, f32[16,32,384]{2,1,0:T(8,128)}) custom-call(f32[24,16,768]{2,1,0:T(8,128)S(1)} %get-tuple-element.13.pm, f32[24,16,768]{2,1,0:T(8,128)S(1)} %get-tuple-element.14.pn, f32[16,32,384]{2,1,0:T(8,128)S(1)} %get-tuple-element.15.tf, ...), custom_call_target="tpu_custom_call" | custom-call | tf_op jit(solution)/shard_map/pallas_call | solution.py:593

commit v5 on v3

--- a/solution.py
+++ b/solution.py
@@ -222,13 +222,13 @@
     m_z = Faces(along_gx, cut_all(pm.at[0], pm.at[planes - 1], lanes), hz_m, recv, 2 * chunks)
     m_x = Faces(along_gy, cut_all(fx_m.at[0], fx_m.at[1], lanes), hx_m, recv, 3 * chunks)
     at = 4 * chunks
-    e_z = Faces(along_gx, cut_all(fz_e.at[0], fz_e.at[1], depths), hz_e, recv, at, True)
-    e_x = Faces(along_gy, cut_all(fx_e.at[0], fx_e.at[1], depths), hx_e, recv, at + 1, True)
+    e_z = Faces(along_gx, cut_all(fz_e.at[0], fz_e.at[1], depths), hz_e, recv, 2 * chunks, True)
+    e_x = Faces(along_gy, cut_all(fx_e.at[0], fx_e.at[1], depths), hx_e, recv, 3 * chunks, True)
     uw_z = Faces(along_gx, both_of(
-        (u_in.at[0], w_in.at[0]), (u_in.at[tile_rows - 1], w_in.at[tile_rows - 1])), hz_uw, recv, at + 2, True)
+        (u_in.at[0], w_in.at[0]), (u_in.at[tile_rows - 1], w_in.at[tile_rows - 1])), hz_uw, recv, at, True)
     uw_x = Faces(along_gy, both_of(
         (u_in.at[:, 0, :], w_in.at[:, 0, :]),
-        (u_in.at[:, tile_cols - 1, :], w_in.at[:, tile_cols - 1, :])), hx_uw, recv, at + 3, True)
+        (u_in.at[:, tile_cols - 1, :], w_in.at[:, tile_cols - 1, :])), hx_uw, recv, at + 1, True)
 
     faces_in[1].wait()
     pl.semaphore_wait(barrier, along_gx.neighbours + along_gy.neighbours)
@@ -583,7 +583,7 @@
             wave_z, wave_x, wave_z, wave_x,
             pltpu.VMEM((2, 2) + tile[1:], F32), pltpu.VMEM((2, 2, tile[0], tile[2]), F32), cell_z, cell_x,
             cell, pltpu.VMEM((planes // 2 * rows + 2 * planes, lateral), F32), wave_x, lines, lines,
-            dma((2,)), dma((2,)), dma((4 * chunks + 4,)), dma((chunks,)), dma((chunks,)), regular((2,)), regular((2,))],
+            dma((2,)), dma((2,)), dma((4 * chunks + 2,)), dma((chunks,)), dma((chunks,)), regular((2,)), regular((2,))],
         compiler_params=pltpu.CompilerParams(
             collective_id=0, has_side_effects=True, vmem_limit_bytes=58 * 1024 * 1024),
     )(pressure, pressure_prev, courant, nonlinearity, absorption, own_map.T, slot_table.T,

time: 22.6 us -> 22.6 us (level)
  no operation moved by 1% of the time
where the time goes in v5:
time: 22.6 us; the launch traced here: 22.2 us
  Pallas kernels  21.6 us (96%)
  between operations  0.64 us (3%)
    pallas_call x1, Pallas kernels, local(): pl.pallas_call(functools.partial(kernel, capacity, slots, width), out_sha...  19.3 us
    pallas_call x1, Pallas kernels, local(): pl.pallas_call(finish, out_shape=waves + cells * 3, in_specs=[vmem] * 8,...  2.22 us

profile of v5, /device:TPU:0, one launch (start us, length us, event | category | flops | bytes accessed | tf_op | source)
XLA Modules:
  0.0 22.2 jit_solution(6065335209070830560)
XLA Ops:
  0.6 19.3 %shard_map.155 = (f32[24,16,768]{2,1,0:T(8,128)S(1)}, f32[24,16,768]{2,1,0:T(8,128)S(1)}, f32[16,32,384]{2,1,0:T(8,128)S(1)}, f32[16,32,384]{2,1,0:T(8,128)S(1)}...) custom-call(f32[24,16,768]{2,1,0:T(8,128)} %p_in.1, ...), custom_call_target="tpu_custom_call" | custom-call | tf_op jit(solution)/shard_map/pallas_call | solution.py:573
  20.0 2.2 %shard_map.156 = (f32[24,16,768]{2,1,0:T(8,128)}, f32[24,16,768]{2,1,0:T(8,128)}, f32[16,32,384]{2,1,0:T(8,128)}, f32[16,32,384]{2,1,0:T(8,128)}, f32[16,32,384]{2,1,0:T(8,128)}) custom-call(f32[24,16,768]{2,1,0:T(8,128)S(1)} %get-tuple-element.13.pm, f32[24,16,768]{2,1,0:T(8,128)S(1)} %get-tuple-element.14.pn, f32[16,32,384]{2,1,0:T(8,128)S(1)} %get-tuple-element.15.tf, ...), custom_call_target="tpu_custom_call" | custom-call | tf_op jit(solution)/shard_map/pallas_call | solution.py:591

commit v6 on v3

--- a/solution.py
+++ b/solution.py
@@ -150,7 +150,7 @@
     fields, now_before, k, tables, layers, load,
     faces_p, sides, fx_m, fx_n, fz_e, fx_e,
     hz_p, hx_p, hz_m, hx_m, hz_uw, hx_uw, hz_e, hx_e,
-    rest, paired, gain, packed, got,
+    rest, paired, gain, gain_z, packed, got,
     sent_z, sent_x, recv, line_send, line_recv, token_z, token_x,
 ):
     _, planes, rows, lateral = fields.shape
@@ -359,6 +359,8 @@
     paired[pair_at(last), :] = second(planes - 2, pm[planes - 3], pm[planes - 1]) + second(
         planes - 1, pm[planes - 2], None)
     gain[...] = 0.1 * sides[2:4] * lax.rsqrt(sides[0:2])
+    for side, z in ((0, 0), (1, planes - 1)):
+        gain_z[side] = 0.1 * a[z] * lax.rsqrt(c[z])
 
     used = [pl.ds(0, capacity + 1)] + [pl.ds(0, capacity)] * (chunks - 1)
     others = pl.ds(0, blocks - 1)
@@ -411,7 +413,7 @@
             fx_n[1, z:z + 1, at] = new[-1:]
             where = slice(pair * rows, (pair + 1) * rows)
             paired[where, at] = paired[where, at] + (
-                0.1 * a[z, :, at] * lax.rsqrt(c[z, :, at]) * (extra * (2.0 * old + extra)))
+                gain_z[side, :, at] * (extra * (2.0 * old + extra)))
         for side in range(2):
             old = fx_n[side, :, at]
             extra = sides[side, :, at] * hx_m[side, :, at]
@@ -420,8 +422,8 @@
                 gain[side, :, at] * (extra * (2.0 * old + extra)))
         high, low = split(paired[:, at])
         coarse = dot(high, lanes_two) + dot(low, lanes_two)
-        high, low = split(coarse)
-        coarse = (dot(match, high) + dot(match, low)).reshape(blocks, slots, half)
+        coarse = dot(match, jnp.concatenate(split(coarse), axis=1))
+        coarse = (coarse[:, :half] + coarse[:, half:]).reshape(blocks, slots, half)
         if i == 0:
             coarse = jnp.where(iota(coarse.shape, 1) == capacity, places, coarse)
             along_gy.close()
@@ -582,7 +584,7 @@
             wave_x, wave_x, cell_z, cell_x,
             wave_z, wave_x, wave_z, wave_x,
             pltpu.VMEM((2, 2) + tile[1:], F32), pltpu.VMEM((2, 2, tile[0], tile[2]), F32), cell_z, cell_x,
-            cell, pltpu.VMEM((planes // 2 * rows + 2 * planes, lateral), F32), wave_x, lines, lines,
+            cell, pltpu.VMEM((planes // 2 * rows + 2 * planes, lateral), F32), wave_x, wave_z, lines, lines,
             dma((2,)), dma((2,)), dma((4 * chunks + 4,)), dma((chunks,)), dma((chunks,)), regular((2,)), regular((2,))],
         compiler_params=pltpu.CompilerParams(
             collective_id=0, has_side_effects=True, vmem_limit_bytes=58 * 1024 * 1024),

time: 22.6 us -> 22.6 us (level)
  no operation moved by 1% of the time
where the time goes in v6:
time: 22.6 us; the launch traced here: 22.2 us
  Pallas kernels  21.6 us (96%)
  between operations  0.64 us (3%)
    pallas_call x1, Pallas kernels, local(): pl.pallas_call(functools.partial(kernel, capacity, slots, width), out_sha...  19.3 us
    pallas_call x1, Pallas kernels, local(): pl.pallas_call(finish, out_shape=waves + cells * 3, in_specs=[vmem] * 8,...  2.22 us

profile of v6, /device:TPU:0, one launch (start us, length us, event | category | flops | bytes accessed | tf_op | source)
XLA Modules:
  0.0 22.2 jit_solution(12348508429619644342)
XLA Ops:
  0.6 19.3 %shard_map.155 = (f32[24,16,768]{2,1,0:T(8,128)S(1)}, f32[24,16,768]{2,1,0:T(8,128)S(1)}, f32[16,32,384]{2,1,0:T(8,128)S(1)}, f32[16,32,384]{2,1,0:T(8,128)S(1)}...) custom-call(f32[24,16,768]{2,1,0:T(8,128)} %p_in.1, ...), custom_call_target="tpu_custom_call" | custom-call | tf_op jit(solution)/shard_map/pallas_call | solution.py:575
  20.0 2.2 %shard_map.156 = (f32[24,16,768]{2,1,0:T(8,128)}, f32[24,16,768]{2,1,0:T(8,128)}, f32[16,32,384]{2,1,0:T(8,128)}, f32[16,32,384]{2,1,0:T(8,128)}, f32[16,32,384]{2,1,0:T(8,128)}) custom-call(f32[24,16,768]{2,1,0:T(8,128)S(1)} %get-tuple-element.13.pm, f32[24,16,768]{2,1,0:T(8,128)S(1)} %get-tuple-element.14.pn, f32[16,32,384]{2,1,0:T(8,128)S(1)} %get-tuple-element.15.tf, ...), custom_call_target="tpu_custom_call" | custom-call | tf_op jit(solution)/shard_map/pallas_call | solution.py:593
